TPU v7x, 16 devices: a whole 2x2x2 slice. The times are simulated.
16 devices in a mesh: fsdp: 16 (over z, y, x, core).
Axes of the slice: x: 2, y: 2, z: 2, core: 2. Of those that a mesh axis runs over, the one named last changes fastest.
Arguments:
- hidden: bfloat16 [16, 128, 1024], P('fsdp')
- grad_out: bfloat16 [16, 128, 1024], P('fsdp')
- positions: int32 [16, 128], P('fsdp')
- norm1_gain: bfloat16 [1024], P('fsdp')
- norm2_gain: bfloat16 [1024], P('fsdp')
- q_norm_gain: bfloat16 [128], replicated
- k_norm_gain: bfloat16 [128], replicated
- w_q: bfloat16 [1024, 2048], P('fsdp')
- w_k: bfloat16 [1024, 1024], P('fsdp')
- w_v: bfloat16 [1024, 1024], P('fsdp')
- w_o: bfloat16 [2048, 1024], P('fsdp')
- w_gate: bfloat16 [1024, 3072], P('fsdp')
- w_up: bfloat16 [1024, 3072], P('fsdp')
- w_down: bfloat16 [3072, 1024], P('fsdp')
Outputs:
- output 1: bfloat16 [16, 128, 1024], P('fsdp')
- output 2: bfloat16 [16, 128, 1024], P('fsdp')
- output 3: float32 [1024], P('fsdp')
- output 4: float32 [1024], P('fsdp')
- output 5: float32 [128], replicated
- output 6: float32 [128], replicated
- output 7: float32 [1024, 2048], P('fsdp')
- output 8: float32 [1024, 1024], P('fsdp')
- output 9: float32 [1024, 1024], P('fsdp')
- output 10: float32 [2048, 1024], P('fsdp')
- output 11: float32 [1024, 3072], P('fsdp')
- output 12: float32 [1024, 3072], P('fsdp')
- output 13: float32 [3072, 1024], P('fsdp')
All inputs are finite; a program needn't handle non-finite values.
Results may differ from a plain program's by a relative error of at most 0.02.
Values are sent between devices in bfloat16 or wider.
A program may use at most 1 GiB of HBM per device.

v0:
```python
import jax
import jax.numpy as jnp
from jax import lax
from jax.sharding import PartitionSpec as P

RMS_EPS = 1e-6
ROPE_THETA = 1000000.0


def rms_scale(tensor):
    return lax.rsqrt(jnp.mean(tensor * tensor, axis=-1, keepdims=True) + RMS_EPS)


def norm_backward(d_unit, unit_val, scale_val):
    return scale_val * (d_unit - unit_val * jnp.mean(d_unit * unit_val, axis=-1, keepdims=True))


def rotate_half(tensor):
    half_dim = tensor.shape[-1] // 2
    return jnp.concatenate([-tensor[..., half_dim:], tensor[..., :half_dim]], axis=-1)


def matmul(left_op, right_op):
    return jnp.dot(left_op, right_op, preferred_element_type=jnp.float32)


def matmul_tn(left_op, right_op):
    return lax.dot_general(left_op, right_op, (((0,), (0,)), ((), ())), preferred_element_type=jnp.float32)


def matmul_nt(left_op, right_op):
    return lax.dot_general(left_op, right_op, (((1,), (1,)), ((), ())), preferred_element_type=jnp.float32)


def rope_tables(positions, head_dim):
    inv_freq = ROPE_THETA ** (-2.0 * jnp.arange(head_dim // 2, dtype=jnp.float32) / head_dim)
    rope_angle = positions.reshape(-1, 1).astype(jnp.float32) * inv_freq
    cos_half = jnp.cos(rope_angle)
    sin_half = jnp.sin(rope_angle)
    cos_t = jnp.concatenate([cos_half, cos_half], axis=-1)[:, None, :]
    sin_t = jnp.concatenate([sin_half, sin_half], axis=-1)[:, None, :]
    return cos_t, sin_t


def head_norm_rope(projected, num_heads, head_dim, gain_vec, cos_t, sin_t):
    heads_float = projected.reshape(projected.shape[0], num_heads, head_dim).astype(jnp.float32)
    head_scale = rms_scale(heads_float)
    head_unit = heads_float * head_scale
    scaled = head_unit * gain_vec.astype(jnp.float32)
    rotated = (scaled * cos_t + rotate_half(scaled) * sin_t).astype(jnp.bfloat16)
    return rotated, head_unit, head_scale


def head_norm_rope_backward(d_rotated, head_unit, head_scale, gain_vec, cos_t, sin_t):
    d_scaled = d_rotated * cos_t - rotate_half(d_rotated * sin_t)
    d_gain = jnp.sum(d_scaled * head_unit, axis=(0, 1))
    d_projected = norm_backward(d_scaled * gain_vec.astype(jnp.float32), head_unit, head_scale)
    return d_projected.reshape(d_projected.shape[0], -1).astype(jnp.bfloat16), d_gain


def forward_local(hidden, positions, weights):
    norm1_gain, norm2_gain, q_norm_gain, k_norm_gain, w_q, w_k, w_v, w_o, w_gate, w_up, w_down = weights
    batch_local, seq_len, model_width = hidden.shape
    head_dim = q_norm_gain.shape[0]
    num_heads = w_q.shape[1] // head_dim
    kv_heads = w_k.shape[1] // head_dim
    tokens = batch_local * seq_len
    x_float = hidden.reshape(tokens, model_width).astype(jnp.float32)
    x_scale = rms_scale(x_float)
    x_unit = x_float * x_scale
    normed = (x_unit * norm1_gain.astype(jnp.float32)).astype(jnp.bfloat16)
    q_proj = matmul(normed, w_q).astype(jnp.bfloat16)
    k_proj = matmul(normed, w_k).astype(jnp.bfloat16)
    v_proj = matmul(normed, w_v).astype(jnp.bfloat16)
    cos_t, sin_t = rope_tables(positions, head_dim)
    q_rot, q_unit, q_scale = head_norm_rope(q_proj, num_heads, head_dim, q_norm_gain, cos_t, sin_t)
    k_rot, k_unit, k_scale = head_norm_rope(k_proj, kv_heads, head_dim, k_norm_gain, cos_t, sin_t)
    q_grouped = q_rot.reshape(batch_local, seq_len, kv_heads, num_heads // kv_heads, head_dim)
    k_seq = k_rot.reshape(batch_local, seq_len, kv_heads, head_dim)
    v_seq = v_proj.reshape(batch_local, seq_len, kv_heads, head_dim)
    scores = jnp.einsum("bskgd,btkd->bksgt", q_grouped, k_seq, preferred_element_type=jnp.float32) * (head_dim ** -0.5)
    causal = (jnp.arange(seq_len)[:, None] >= jnp.arange(seq_len)[None, :])[:, None, :]
    attn_probs = jax.nn.softmax(jnp.where(causal, scores, -1e30), axis=-1)
    attn_ctx = jnp.einsum("bksgt,btkd->bskgd", attn_probs.astype(jnp.bfloat16), v_seq, preferred_element_type=jnp.float32).astype(jnp.bfloat16).reshape(tokens, num_heads * head_dim)
    attn_out = matmul(attn_ctx, w_o).astype(jnp.bfloat16)
    resid_float = (x_float + attn_out.astype(jnp.float32)).astype(jnp.bfloat16).astype(jnp.float32)
    r_scale = rms_scale(resid_float)
    r_unit = resid_float * r_scale
    mlp_in = (r_unit * norm2_gain.astype(jnp.float32)).astype(jnp.bfloat16)
    gate_proj = matmul(mlp_in, w_gate).astype(jnp.bfloat16)
    up_proj = matmul(mlp_in, w_up).astype(jnp.bfloat16)
    mlp_act = (jax.nn.silu(gate_proj.astype(jnp.float32)) * up_proj.astype(jnp.float32)).astype(jnp.bfloat16)
    down_proj = matmul(mlp_act, w_down).astype(jnp.bfloat16)
    layer_out = (resid_float + down_proj.astype(jnp.float32)).astype(jnp.bfloat16).reshape(batch_local, seq_len, model_width)
    saved_acts = {"x_unit": x_unit, "x_scale": x_scale, "normed": normed, "cos_t": cos_t, "sin_t": sin_t, "q_unit": q_unit, "q_scale": q_scale, "k_unit": k_unit, "k_scale": k_scale, "q_grouped": q_grouped, "k_seq": k_seq, "v_seq": v_seq, "attn_probs": attn_probs, "attn_ctx": attn_ctx, "r_unit": r_unit, "r_scale": r_scale, "mlp_in": mlp_in, "gate_proj": gate_proj, "up_proj": up_proj, "mlp_act": mlp_act}
    return layer_out, saved_acts


def backward_local(grad_out, saved_acts, weights):
    norm1_gain, norm2_gain, q_norm_gain, k_norm_gain, w_q, w_k, w_v, w_o, w_gate, w_up, w_down = weights
    batch_local, seq_len, model_width = grad_out.shape
    tokens = batch_local * seq_len
    q_grouped = saved_acts["q_grouped"]
    kv_heads = q_grouped.shape[2]
    kv_group = q_grouped.shape[3]
    head_dim = q_grouped.shape[4]
    num_heads = kv_heads * kv_group
    dy_flat = grad_out.reshape(tokens, model_width)
    grad_down = matmul_tn(saved_acts["mlp_act"], dy_flat)
    d_mlp_act = matmul_nt(dy_flat, w_down)
    gate_float = saved_acts["gate_proj"].astype(jnp.float32)
    gate_sig = jax.nn.sigmoid(gate_float)
    d_up_proj = (d_mlp_act * gate_float * gate_sig).astype(jnp.bfloat16)
    d_gate_proj = (d_mlp_act * saved_acts["up_proj"].astype(jnp.float32) * gate_sig * (1.0 + gate_float * (1.0 - gate_sig))).astype(jnp.bfloat16)
    grad_gate = matmul_tn(saved_acts["mlp_in"], d_gate_proj)
    grad_up = matmul_tn(saved_acts["mlp_in"], d_up_proj)
    d_mlp_in = matmul_nt(d_gate_proj, w_gate) + matmul_nt(d_up_proj, w_up)
    grad_norm2 = jnp.sum(d_mlp_in * saved_acts["r_unit"], axis=0)
    d_resid = dy_flat.astype(jnp.float32) + norm_backward(d_mlp_in * norm2_gain.astype(jnp.float32), saved_acts["r_unit"], saved_acts["r_scale"])
    d_resid_bf = d_resid.astype(jnp.bfloat16)
    grad_wo = matmul_tn(saved_acts["attn_ctx"], d_resid_bf)
    d_attn_ctx = matmul_nt(d_resid_bf, w_o).astype(jnp.bfloat16).reshape(batch_local, seq_len, kv_heads, kv_group, head_dim)
    attn_probs = saved_acts["attn_probs"]
    d_value = jnp.einsum("bksgt,bskgd->btkd", attn_probs.astype(jnp.bfloat16), d_attn_ctx, preferred_element_type=jnp.float32).astype(jnp.bfloat16).reshape(tokens, kv_heads * head_dim)
    d_probs = jnp.einsum("bskgd,btkd->bksgt", d_attn_ctx, saved_acts["v_seq"], preferred_element_type=jnp.float32)
    d_scores = attn_probs * (d_probs - jnp.sum(attn_probs * d_probs, axis=-1, keepdims=True))
    d_scores = (d_scores * (head_dim ** -0.5)).astype(jnp.bfloat16)
    d_q_rot = jnp.einsum("bksgt,btkd->bskgd", d_scores, saved_acts["k_seq"], preferred_element_type=jnp.float32).reshape(tokens, num_heads, head_dim)
    d_k_rot = jnp.einsum("bksgt,bskgd->btkd", d_scores, q_grouped, preferred_element_type=jnp.float32).reshape(tokens, kv_heads, head_dim)
    d_query, grad_qgain = head_norm_rope_backward(d_q_rot, saved_acts["q_unit"], saved_acts["q_scale"], q_norm_gain, saved_acts["cos_t"], saved_acts["sin_t"])
    d_key, grad_kgain = head_norm_rope_backward(d_k_rot, saved_acts["k_unit"], saved_acts["k_scale"], k_norm_gain, saved_acts["cos_t"], saved_acts["sin_t"])
    normed = saved_acts["normed"]
    grad_wq = matmul_tn(normed, d_query)
    grad_wk = matmul_tn(normed, d_key)
    grad_wv = matmul_tn(normed, d_value)
    d_normed = matmul_nt(d_query, w_q) + matmul_nt(d_key, w_k) + matmul_nt(d_value, w_v)
    grad_norm1 = jnp.sum(d_normed * saved_acts["x_unit"], axis=0)
    d_hidden = (d_resid + norm_backward(d_normed * norm1_gain.astype(jnp.float32), saved_acts["x_unit"], saved_acts["x_scale"])).astype(jnp.bfloat16)
    local_grads = (grad_norm1, grad_norm2, grad_qgain, grad_kgain, grad_wq, grad_wk, grad_wv, grad_wo, grad_gate, grad_up, grad_down)
    return d_hidden.reshape(batch_local, seq_len, model_width), local_grads


def solution(mesh):
    axis_name = mesh.axis_names[0]
    group_size = mesh.shape[axis_name]
    sharded = P(axis_name)
    in_specs = (sharded, sharded, sharded, sharded, sharded, P(), P()) + (sharded,) * 7
    out_specs = (sharded, sharded, sharded, sharded, P(), P()) + (sharded,) * 7

    def gather_weights(row_shards, q_norm_gain, k_norm_gain):
        full_rows = tuple(lax.all_gather(row_shard, axis_name, axis=0, tiled=True) for row_shard in row_shards)
        return (full_rows[0], full_rows[1], q_norm_gain, k_norm_gain) + full_rows[2:]

    def device_step(hidden, grad_out, positions, norm1_gain, norm2_gain, q_norm_gain, k_norm_gain, w_q, w_k, w_v, w_o, w_gate, w_up, w_down):
        row_shards = (norm1_gain, norm2_gain, w_q, w_k, w_v, w_o, w_gate, w_up, w_down)
        weights_fwd = gather_weights(row_shards, q_norm_gain, k_norm_gain)
        layer_out, saved_acts = forward_local(hidden, positions, weights_fwd)
        layer_out, row_shards = lax.optimization_barrier((layer_out, row_shards))
        weights_bwd = gather_weights(row_shards, q_norm_gain, k_norm_gain)
        d_hidden, local_grads = backward_local(grad_out, saved_acts, weights_bwd)
        inv_tokens = 1.0 / (hidden.shape[0] * hidden.shape[1] * group_size)
        row_grads = local_grads[:2] + local_grads[4:]
        reduced = tuple(lax.psum_scatter(row_grad * inv_tokens, axis_name, scatter_dimension=0, tiled=True) for row_grad in row_grads)
        qgain_sum = lax.psum(local_grads[2] * inv_tokens, axis_name)
        kgain_sum = lax.psum(local_grads[3] * inv_tokens, axis_name)
        return (layer_out, d_hidden, reduced[0], reduced[1], qgain_sum, kgain_sum) + reduced[2:]

    return jax.shard_map(device_step, mesh=mesh, in_specs=in_specs, out_specs=out_specs, check_vma=False)
```

profile of v0, /device:TPU:0, one launch (start us, length us, event | category | flops | bytes accessed | tf_op | source)
XLA Modules:
  0.0 1164.9 jit_solution(17491292851248443951)
XLA Ops:
  13.6 34.8 %all-reduce.8 = (bf16[1024]{0:T(1024)(128)(2,1)S(1)}, bf16[1024]{0:T(1024)(128)(2,1)S(1)}) all-reduce(bf16[1024]{0:T(1024)(128)(2,1)S(1)} %dynamic-update-slice, bf16[1024]{0:T(1024)(128)(2,1)S(1)} %dynamic-update-slice.1), channel_id=1, replica_groups=mesh['fsdp'=16] {'fsdp'}, use_global_device_ids=true, to_apply=%add | all-reduce | flops 2048 | bytes 8192
  53.0 2.2 fusion.17
  56.5 15.8 %all-gather.15.cloned.1.call-done = bf16[1024,1024]{1,0:T(8,128)(2,1)} async-done(((bf16[64,1024]{1,0:T(8,128)(2,1)}), bf16[1024,1024]{1,0:T(8,128)(2,1)}) %all-gather.15.cloned.1.call-update) | async-done | bytes 2097168 | tf_op jit(solution)/shard_map/all_gather | solution.py:151
  76.2 33.4 %all-gather.17.cloned.1.call-done = bf16[1024,2048]{1,0:T(8,128)(2,1)} async-done(((bf16[64,2048]{1,0:T(8,128)(2,1)}), bf16[1024,2048]{1,0:T(8,128)(2,1)}) %all-gather.17.cloned.1.call-update) | async-done | bytes 4194320 | tf_op jit(solution)/shard_map/all_gather | solution.py:151
  109.7 3.0 fusion.4
  115.1 2.6 fusion.87
  119.4 27.4 %all-gather.21.cloned.1.call-done = bf16[2048,1024]{1,0:T(8,128)(2,1)} async-done(((bf16[128,1024]{1,0:T(8,128)(2,1)}), bf16[2048,1024]{1,0:T(8,128)(2,1)}) %all-gather.21.cloned.1.call-update) | async-done | bytes 4194320 | tf_op jit(solution)/shard_map/all_gather | solution.py:151
  146.8 3.0 multiply_reduce_fusion.8
  151.2 39.5 %all-gather.23.cloned.1.call-done = bf16[1024,3072]{1,0:T(8,128)(2,1)} async-done(((bf16[64,3072]{1,0:T(8,128)(2,1)}), bf16[1024,3072]{1,0:T(8,128)(2,1)}) %all-gather.23.cloned.1.call-update) | async-done | bytes 6291472 | tf_op jit(solution)/shard_map/all_gather | solution.py:151
  190.7 5.0 fusion.3
  195.7 38.9 %all-gather.25.cloned.1.call-done = bf16[1024,3072]{1,0:T(8,128)(2,1)} async-done(((bf16[64,3072]{1,0:T(8,128)(2,1)}), bf16[1024,3072]{1,0:T(8,128)(2,1)}) %all-gather.25.cloned.1.call-update) | async-done | bytes 6291472 | tf_op jit(solution)/shard_map/all_gather | solution.py:151
  234.6 5.8 multiply_convert_fusion.2
  240.4 38.2 %all-gather.27.cloned.1.call-done = bf16[3072,1024]{1,0:T(8,128)(2,1)} async-done(((bf16[192,1024]{1,0:T(8,128)(2,1)}), bf16[3072,1024]{1,0:T(8,128)(2,1)}) %all-gather.27.cloned.1.call-update) | async-done | bytes 6291472 | tf_op jit(solution)/shard_map/all_gather | solution.py:151
  278.6 4.8 fusion.23
  287.6 7.5 convolution_multiply_fusion
  300.2 32.2 %all-reduce.7 = (bf16[1024]{0:T(1024)(128)(2,1)S(1)}, bf16[1024]{0:T(1024)(128)(2,1)}) all-reduce(bf16[1024]{0:T(1024)(128)(2,1)S(1)} %dynamic-update-slice.2, bf16[1024]{0:T(1024)(128)(2,1)S(1)} %dynamic-update-slice.3), channel_id=1, replica_groups=mesh['fsdp'=16] {'fsdp'}, use_global_device_ids=true, to_apply=%add.2 | all-reduce | flops 2048 | bytes 8192
  333.0 7.3 multiply_convert_fusion
  340.3 29.9 %all-gather.31.cloned.1.call-done = bf16[1024,3072]{1,0:T(8,128)(2,1)} async-done(((bf16[64,3072]{1,0:T(8,128)(2,1)}), bf16[1024,3072]{1,0:T(8,128)(2,1)}) %all-gather.31.cloned.1.call-update) | async-done | bytes 6291472 | tf_op jit(solution)/shard_map/all_gather | solution.py:151
  370.2 5.3 fusion.90
  375.5 38.6 %all-gather.33.cloned.1.call-done = bf16[1024,3072]{1,0:T(8,128)(2,1)} async-done(((bf16[64,3072]{1,0:T(8,128)(2,1)}), bf16[1024,3072]{1,0:T(8,128)(2,1)}) %all-gather.33.cloned.1.call-update) | async-done | bytes 6291472 | tf_op jit(solution)/shard_map/all_gather | solution.py:151
  414.1 5.9 multiply_reduce_fusion.5
  420.2 31.2 %all-gather.35.cloned.1.call-done = bf16[2048,1024]{1,0:T(8,128)(2,1)} async-done(((bf16[128,1024]{1,0:T(8,128)(2,1)}), bf16[2048,1024]{1,0:T(8,128)(2,1)}) %all-gather.35.cloned.1.call-update) | async-done | bytes 4194320 | tf_op jit(solution)/shard_map/all_gather | solution.py:151
  451.4 3.7 convolution_convert_fusion.2
  456.1 2.4 fusion.71
  458.6 3.9 bitcast_multiply_fusion.5
  463.6 2.5 multiply_reduce_fusion.4
  472.4 3.6 convolution_multiply_fusion.6
  477.6 2.8 convolution_multiply_fusion.5
  483.5 2.8 fusion.31
  490.7 2.4 copy.161
  493.1 2.4 copy.162
  501.5 2.6 fusion.26
  504.1 4.6 convolution_multiply_fusion.4
  509.9 6.4 convolution_multiply_fusion.2
  517.4 6.4 convolution_multiply_fusion.1
  525.0 4.5 convolution_multiply_fusion.3
  530.5 2.4 fusion.91
  533.0 2.4 fusion.92
  535.4 14.2 %all-gather.37.cloned.1.call-done = bf16[1024,2048]{1,0:T(8,128)(2,1)} async-done(((bf16[64,2048]{1,0:T(8,128)(2,1)}), bf16[1024,2048]{1,0:T(8,128)(2,1)}) %all-gather.37.cloned.1.call-update) | async-done | bytes 4194320 | tf_op jit(solution)/shard_map/all_gather | solution.py:151
  549.6 3.8 fusion.48
  553.5 32.1 %all-reduce.6 = (f32[1024]{0:T(1024)S(1)}, f32[1024]{0:T(1024)S(1)}, f32[128]{0:T(128)}, f32[128]{0:T(128)}) all-reduce(f32[1024]{0:T(1024)S(1)} %broadcast_multiply_fusion.3, f32[1024]{0:T(1024)S(1)} %broadcast_multiply_fusion.2, f32[128]{0:T(128)S(1)} %broadcast_multiply_fusion.6, ...), channel_id=2, replica_groups=mesh['fsdp'=16] {'fsdp'}, use_global_device_ids=true, to_apply=%region_12.13.clone | all-reduce | flops 2304 | bytes 18432
  587.7 57.4 %reduce-scatter.20.cloned.1.call-done = f32[192,1024]{1,0:T(8,128)} async-done(((f32[3072,1024]{1,0:T(8,128)}), f32[192,1024]{1,0:T(8,128)}) %reduce-scatter.20.cloned.1.call-update) | async-done | bytes 786448 | tf_op jit(solution)/shard_map/reduce_scatter | solution.py:163
  645.1 66.5 %reduce-scatter.10.cloned.1.call-done = f32[64,1024]{1,0:T(8,128)} async-done(((f32[1024,1024]{1,0:T(8,128)}), f32[64,1024]{1,0:T(8,128)}) %reduce-scatter.10.cloned.1.call-update) | async-done | bytes 262160 | tf_op jit(solution)/shard_map/reduce_scatter | solution.py:163
  711.6 66.0 %reduce-scatter.12.cloned.1.call-done = f32[64,1024]{1,0:T(8,128)} async-done(((f32[1024,1024]{1,0:T(8,128)}), f32[64,1024]{1,0:T(8,128)}) %reduce-scatter.12.cloned.1.call-update) | async-done | bytes 262160 | tf_op jit(solution)/shard_map/reduce_scatter | solution.py:163
  777.6 95.0 %reduce-scatter.8.cloned.1.call-done = f32[64,2048]{1,0:T(8,128)} async-done(((f32[1024,2048]{1,0:T(8,128)}), f32[64,2048]{1,0:T(8,128)}) %reduce-scatter.8.cloned.1.call-update) | async-done | bytes 524304 | tf_op jit(solution)/shard_map/reduce_scatter | solution.py:163
  872.6 93.9 %reduce-scatter.16.cloned.1.call-done = f32[64,3072]{1,0:T(8,128)} async-done(((f32[1024,3072]{1,0:T(8,128)}), f32[64,3072]{1,0:T(8,128)}) %reduce-scatter.16.cloned.1.call-update) | async-done | bytes 786448 | tf_op jit(solution)/shard_map/reduce_scatter | solution.py:163
  966.5 95.5 %reduce-scatter.18.cloned.1.call-done = f32[64,3072]{1,0:T(8,128)} async-done(((f32[1024,3072]{1,0:T(8,128)}), f32[64,3072]{1,0:T(8,128)}) %reduce-scatter.18.cloned.1.call-update) | async-done | bytes 786448 | tf_op jit(solution)/shard_map/reduce_scatter | solution.py:163
  1062.0 95.6 %reduce-scatter.14.cloned.1.call-done = f32[128,1024]{1,0:T(8,128)} async-done(((f32[2048,1024]{1,0:T(8,128)}), f32[128,1024]{1,0:T(8,128)}) %reduce-scatter.14.cloned.1.call-update) | async-done | bytes 524304 | tf_op jit(solution)/shard_map/reduce_scatter | solution.py:163
  (197 shorter events, 61.4 us)
Async XLA Ops:
  7.2 65.2 %copy-start = (bf16[1,128,1024]{2,1,0:T(8,128)(2,1)S(1)}, bf16[1,128,1024]{2,1,0:T(8,128)(2,1)}, u32[]{:S(2)}) copy-start(bf16[1,128,1024]{2,1,0:T(8,128)(2,1)} %param.14) | copy-start | bytes 786436
  7.2 45.8 %all-gather.19.cloned.1.call-start = ((), (), s32[]{:S(2)}) async-start(), calls=%async_computation.9 | async-start | bytes 2228224 | tf_op jit(solution)/shard_map/all_gather | solution.py:151
  7.9 64.4 %all-gather.15.cloned.1.call-start = ((), (), s32[]{:S(2)}) async-start(), calls=%async_computation.7 | async-start | bytes 2228224 | tf_op jit(solution)/shard_map/all_gather | solution.py:151
  8.7 101.0 %all-gather.17.cloned.1.call-start = ((), (), s32[]{:S(2)}) async-start(), calls=%async_computation.8 | async-start | bytes 4456448 | tf_op jit(solution)/shard_map/all_gather | solution.py:151
  9.4 137.4 %all-gather.21.cloned.1.call-start = ((), (), s32[]{:S(2)}) async-start(), calls=%async_computation.10 | async-start | bytes 4456448 | tf_op jit(solution)/shard_map/all_gather | solution.py:151
  10.0 180.7 %all-gather.23.cloned.1.call-start = ((), (), s32[]{:S(2)}) async-start(), calls=%async_computation.11 | async-start | bytes 6684672 | tf_op jit(solution)/shard_map/all_gather | solution.py:151
  10.6 224.0 %all-gather.25.cloned.1.call-start = ((), (), s32[]{:S(2)}) async-start(), calls=%async_computation.12 | async-start | bytes 6684672 | tf_op jit(solution)/shard_map/all_gather | solution.py:151
  11.1 267.5 %all-gather.27.cloned.1.call-start = ((), (), s32[]{:S(2)}) async-start(), calls=%async_computation.13 | async-start | bytes 6684672 | tf_op jit(solution)/shard_map/all_gather | solution.py:151
  11.9 321.1 %all-gather.29.cloned.1.call-start = ((), (), s32[]{:S(2)}) async-start(), calls=%async_computation.14 | async-start | bytes 6684672 | tf_op jit(solution)/shard_map/all_gather | solution.py:151
  49.1 63.9 %copy-start.26 = (f32[128]{0:T(128)}, f32[128]{0:T(128)S(1)}, u32[]{:S(2)}) copy-start(f32[128]{0:T(128)S(1)} %convert_element_type.213) | copy-start | bytes 1540
  49.8 25.6 %copy-start.28 = (f32[128]{0:T(128)}, f32[128]{0:T(128)S(1)}, u32[]{:S(2)}) copy-start(f32[128]{0:T(128)S(1)} %convert_element_type.220) | copy-start | bytes 1540
  53.0 56.6 %copy-start.21 = (f32[128]{0:T(128)}, f32[128]{0:T(128)S(1)}, u32[]{:S(2)}) copy-start(f32[128]{0:T(128)S(1)} %add_rsqrt_fusion.3) | copy-start | bytes 1540
  56.2 20.0 %copy-start.3 = (f32[128,8,128]{0,2,1:T(8,128)}, f32[128,8,128]{0,2,1:T(8,128)S(1)}, u32[]{:S(2)}) copy-start(f32[128,8,128]{0,2,1:T(8,128)S(1)} %copy.147) | copy-start | bytes 1572868
  117.7 29.1 %copy-start.34 = (f32[8,128,2]{1,2,0:T(2,128)}, f32[8,128,2]{1,2,0:T(2,128)S(1)}, u32[]{:S(2)}) copy-start(f32[8,128,2]{1,2,0:T(2,128)S(1)} %get-tuple-element.62) | copy-start | bytes 24580
  119.4 30.4 %copy-start.10 = (bf16[8,128,128,2]{2,1,3,0:T(8,128)(2,1)}, bf16[8,128,128,2]{2,1,3,0:T(8,128)(2,1)S(1)}, u32[]{:S(2)}) copy-start(bf16[8,128,128,2]{2,1,3,0:T(8,128)(2,1)S(1)} %convolution_convert_fusion.4) | copy-start | bytes 1572868
  151.1 83.4 %copy-start.5 = (bf16[128,1024]{1,0:T(8,128)(2,1)}, bf16[128,1024]{1,0:T(8,128)(2,1)S(1)}, u32[]{:S(2)}) copy-start(bf16[128,1024]{1,0:T(8,128)(2,1)S(1)} %multiply_convert_fusion.3) | copy-start | bytes 786436
  278.6 9.0 copy-start.17
  283.4 86.8 %all-gather.31.cloned.1.call-start = ((), (), s32[]{:S(2)}) async-start(), calls=%async_computation.15 | async-start | bytes 6684672 | tf_op jit(solution)/shard_map/all_gather | solution.py:151
  284.2 129.9 %all-gather.33.cloned.1.call-start = ((), (), s32[]{:S(2)}) async-start(), calls=%async_computation.16 | async-start | bytes 6684672 | tf_op jit(solution)/shard_map/all_gather | solution.py:151
  284.7 166.7 %all-gather.35.cloned.1.call-start = ((), (), s32[]{:S(2)}) async-start(), calls=%async_computation.17 | async-start | bytes 4456448 | tf_op jit(solution)/shard_map/all_gather | solution.py:151
  285.5 244.8 %all-gather.39.cloned.1.call-start = ((), (), s32[]{:S(2)}) async-start(), calls=%async_computation.19 | async-start | bytes 2228224 | tf_op jit(solution)/shard_map/all_gather | solution.py:151
  286.1 246.9 %all-gather.41.cloned.1.call-start = ((), (), s32[]{:S(2)}) async-start(), calls=%async_computation.20 | async-start | bytes 2228224 | tf_op jit(solution)/shard_map/all_gather | solution.py:151
  286.8 262.8 %all-gather.37.cloned.1.call-start = ((), (), s32[]{:S(2)}) async-start(), calls=%async_computation.18 | async-start | bytes 4456448 | tf_op jit(solution)/shard_map/all_gather | solution.py:151
  287.4 357.8 %reduce-scatter.20.cloned.1.call-start = ((), (), s32[]{:S(2)}) async-start(), calls=%async_computation.27 | async-start | bytes 13369344 | tf_op jit(solution)/shard_map/reduce_scatter | solution.py:163
  295.1 416.5 %reduce-scatter.10.cloned.1.call-start = ((), (), s32[]{:S(2)}) async-start(), calls=%async_computation.22 | async-start | bytes 4456448 | tf_op jit(solution)/shard_map/reduce_scatter | solution.py:163
  414.1 5.9 copy-start.18
  414.1 5.9 copy-start.23
  414.1 5.9 copy-start.30
  420.2 42.2 %copy-start.1 = (f32[128,1024]{1,0:T(8,128)}, f32[128,1024]{1,0:T(8,128)S(1)}, u32[]{:S(2)}) copy-start(f32[128,1024]{1,0:T(8,128)S(1)} %multiply_add_fusion) | copy-start | bytes 1572868
  456.1 7.5 copy-start.4
  462.5 8.0 copy-start.8
  472.3 3.6 copy-start.14
  472.3 3.7 copy-start.16
  472.4 3.7 copy-start.35
  475.9 1.7 copy-start.22
  476.0 301.7 %reduce-scatter.12.cloned.1.call-start = ((), (), s32[]{:S(2)}) async-start(), calls=%async_computation.23 | async-start | bytes 4456448 | tf_op jit(solution)/shard_map/reduce_scatter | solution.py:163
  477.6 2.9 copy-start.19
  477.6 3.9 copy-start.27
  480.4 392.1 %reduce-scatter.8.cloned.1.call-start = ((), (), s32[]{:S(2)}) async-start(), calls=%async_computation.21 | async-start | bytes 8912896 | tf_op jit(solution)/shard_map/reduce_scatter | solution.py:163
  497.6 3.9 copy-start.24
  499.1 2.4 copy-start.9
  508.7 1.2 copy-start.12
  508.7 457.8 %reduce-scatter.16.cloned.1.call-start = ((), (), s32[]{:S(2)}) async-start(), calls=%async_computation.25 | async-start | bytes 13369344 | tf_op jit(solution)/shard_map/reduce_scatter | solution.py:163
  516.3 545.7 %reduce-scatter.18.cloned.1.call-start = ((), (), s32[]{:S(2)}) async-start(), calls=%async_computation.26 | async-start | bytes 13369344 | tf_op jit(solution)/shard_map/reduce_scatter | solution.py:163
  523.8 1.2 copy-start.11
  523.8 633.8 %reduce-scatter.14.cloned.1.call-start = ((), (), s32[]{:S(2)}) async-start(), calls=%async_computation.24 | async-start | bytes 8912896 | tf_op jit(solution)/shard_map/reduce_scatter | solution.py:163
  529.5 3.4 copy-start.20
  532.9 20.5 %copy-start.25 = (f32[1024]{0:T(1024)S(1)}, f32[1024]{0:T(1024)}, u32[]{:S(2)}) copy-start(f32[1024]{0:T(1024)} %get-tuple-element.37) | copy-start | bytes 12292
  (9 other events, 7.4 us)
Sparse Core Ops, SparseCore 0:
  10.2 31.5 all-gather.18
  44.0 28.2 all-gather.14
  74.6 35.0 all-gather.16
  111.8 35.0 all-gather.20
  148.9 41.7 all-gather.22
  192.8 41.7 all-gather.24
  236.8 41.7 all-gather.26
  283.5 42.6 all-gather.28
  328.5 41.6 all-gather.30
  372.3 41.7 all-gather.32
  416.4 35.0 all-gather.34
  453.5 28.3 all-gather.38
  484.1 28.2 all-gather.40
  514.5 35.0 all-gather.36
  554.7 90.4 reduce-scatter.19
  647.9 63.7 reduce-scatter.9
  714.3 63.2 reduce-scatter.11
  780.3 92.2 reduce-scatter.7
  877.8 88.6 reduce-scatter.15
  971.5 90.4 reduce-scatter.17
  1064.8 92.7 reduce-scatter.13
where the time goes:
time: 1170 us; the launch traced here: 1160 us
  waiting for transfers between devices  885 us (76%)
  matrix products  107 us (9%)
  blocking collectives  99.2 us (8%)
  local copies, waits for them, and re-layouts  30.8 us (3%)
  other arithmetic  25.5 us (2%)
  between operations  15.4 us (1%)
    reduce_scatter x7, waiting for transfers between devices, device_step(): lax.psum_scatter(row_grad * inv_tokens, axis_name, scatter_dimension=0, t...  570 us
    all_gather x14, waiting for transfers between devices, gather_weights(): lax.all_gather(row_shard, axis_name, axis=0, tiled=True)  307 us
    unnamed x3, blocking collectives  99.2 us
    dot_general x7, matrix products, matmul_tn(): lax.dot_general(left_op, right_op, (((0,), (0,)), ((), ())), preferred_el...  35.7 us
    dot_general x7, matrix products, matmul_nt(): lax.dot_general(left_op, right_op, (((1,), (1,)), ((), ())), preferred_el...  30.8 us
    dot_general x7, matrix products, matmul(): return jnp.dot(left_op, right_op, preferred_element_type=jnp.float32)  25.8 us
  transfers between devices with their start and end apart: 21, of which 17 were waited for; matrix products, arithmetic and copies ran while one was open for 13% of the time, Pallas kernels for 0%

commit v1 on v0

v1 whole, which is shorter than its diff:
```python
import jax
import jax.numpy as jnp
from jax import lax
from jax.experimental import pallas as pl
from jax.experimental.pallas import tpu as pltpu
from jax.sharding import PartitionSpec as P

RMS_EPS = 1e-6
ROPE_THETA = 1000000.0
MESH = pl.DeviceIdType.MESH
F32 = jnp.float32
BF16 = jnp.bfloat16
T = 128
D = 1024
NQ = 2048
FF = 3072
HD = 128
Z, Y, X, C = 0, 1, 2, 3
STRIDE = (8, 4, 2, 1)
ALL = slice(None)
VM = pltpu.VMEM
HIGH_VMEM = 67043328


def nn(left_op, right_op):
    return jnp.dot(left_op, right_op, preferred_element_type=F32)


def nt(left_op, right_op):
    return lax.dot_general(left_op, right_op, (((1,), (1,)), ((), ())), preferred_element_type=F32)


def tn(left_op, right_op):
    return lax.dot_general(left_op, right_op, (((0,), (0,)), ((), ())), preferred_element_type=F32)


def rms(val):
    return lax.rsqrt(jnp.mean(val * val, axis=-1, keepdims=True) + RMS_EPS)


def norm_backward(d_unit, unit_val, scale_val):
    return scale_val * (d_unit - unit_val * jnp.mean(d_unit * unit_val, axis=-1, keepdims=True))


class Place:
    def __init__(self):
        self.me = lax.axis_index("fsdp")
        self.bit = [lax.rem(lax.div(self.me, s), 2) for s in STRIDE]

    def near(self, dim):
        return (self.me + STRIDE[dim] * (1 - 2 * self.bit[dim]),)

    def greet(self, dims):
        barrier = pltpu.get_barrier_semaphore()
        for dim in dims:
            pl.semaphore_signal(barrier, inc=1, device_id=self.near(dim), device_id_type=MESH)
        pl.semaphore_wait(barrier, len(dims))


class Spread:
    def __init__(self, place, src, buf, sub, order, axes, sems, part):
        self.place, self.src, self.buf, self.sub, self.order, self.axes = place, src, buf, sub, order, axes
        self.link_send, self.link_recv, self.core_send, self.core_recv, self.local_sem = sems
        self.part, self.last = part, len(order)

    def block(self, full, flip=None):
        index = []
        for dim in self.axes:
            if dim in full:
                index.append(ALL)
            elif dim == flip:
                index.append(1 - self.place.bit[dim])
            else:
                index.append(self.place.bit[dim])
        return self.buf.at[tuple(index) + self.sub]

    def own(self):
        return pltpu.make_async_copy(self.src.at[self.sub], self.block(()), self.local_sem.at[self.part])

    def link(self, step):
        dst = self.block(self.order[:step])
        return pltpu.make_async_remote_copy(
            src_ref=self.src.at[self.sub] if step == 0 else dst,
            dst_ref=dst,
            send_sem=self.link_send.at[self.part, step],
            recv_sem=self.link_recv.at[self.part, step],
            device_id=self.place.near(self.order[step]),
            device_id_type=MESH,
        )

    def core(self, step):
        dst = self.block(()) if step == 0 else self.block(self.order[: step - 1], self.order[step - 1])
        return pltpu.make_async_remote_copy(
            src_ref=self.src.at[self.sub] if step == 0 else dst,
            dst_ref=dst,
            send_sem=self.core_send.at[self.part, step],
            recv_sem=self.core_recv.at[self.part, step],
            device_id=self.place.near(C),
            device_id_type=MESH,
        )

    def begin(self):
        self.link(0).start()
        self.own().start()
        self.core(0).start()

    def advance(self, step):
        if step == 0:
            self.own().wait()
        self.link(step).wait_recv()
        if step + 1 < self.last:
            self.link(step + 1).start()
        self.core(step + 1).start()

    def arrived(self):
        for step in range(self.last + 1):
            self.core(step).wait_recv()

    def drain(self):
        for step in range(self.last):
            self.link(step).wait_send()
        for step in range(self.last + 1):
            self.core(step).wait_send()


class Group:
    def __init__(self, place, third):
        self.place, self.third = place, third
        self.axes = tuple(dim for dim in (Z, Y, X, C) if dim != third)
        bits = [place.bit[dim] for dim in self.axes]
        self.position = 4 * bits[0] + 2 * bits[1] + bits[2]
        chips = [dim for dim in self.axes if dim != C]
        self.orders = (tuple(chips), tuple(chips[::-1]))

    def members(self):
        flips = [(1, 1, 1), (1, 1, 0), (1, 0, 1), (0, 1, 1), (1, 0, 0), (0, 1, 0), (0, 0, 1), (0, 0, 0)]
        for flip in flips:
            bit = list(self.place.bit)
            for dim, turned in zip(self.axes, flip):
                if turned:
                    bit[dim] = 1 - bit[dim]
            yield bit

    def spot(self, bit):
        first, second, third = (bit[dim] for dim in self.axes)
        return 4 * first + 2 * second + third

    def across(self, bit):
        return tuple(ALL if dim == self.third else bit[dim] for dim in range(4))

    def side(self, mine):
        bit = self.place.bit[self.third]
        return tuple((bit if mine else 1 - bit) if dim == self.third else ALL for dim in range(4))


def device_of(bit):
    return (8 * bit[Z] + 4 * bit[Y] + 2 * bit[X] + bit[C],)


class Exchange:
    def __init__(self, group, number, piece, slot, blocks, sems):
        self.group, self.piece, self.slot, self.blocks = group, piece, slot, blocks
        self.send, self.recv, self.local = (sem.at[number] for sem in sems)

    def own(self):
        return pltpu.make_async_copy(self.piece(self.group.place.bit), self.slot, self.local)

    def begin(self):
        *others, _ = self.group.members()
        for bit in others:
            pltpu.make_async_remote_copy(
                src_ref=self.piece(bit),
                dst_ref=self.slot,
                send_sem=self.send,
                recv_sem=self.recv,
                device_id=device_of(bit),
                device_id_type=MESH,
            ).start()
        self.own().start()

    def arrived(self):
        self.own().wait()
        pltpu.make_async_copy(self.blocks, self.blocks, self.recv).wait()

    def drain(self):
        pltpu.make_async_copy(self.blocks, self.blocks, self.send).wait()


ORDERS = ((X, Y, Z), (Y, Z, X), (Z, X, Y))


def head_forward(proj, gain, cos, sin):
    val = proj.astype(F32)
    scaled = val * rms(val) * gain
    return (scaled * cos + pltpu.roll(scaled, 64, axis=1) * sin).astype(BF16)


def head_backward(d_rot, proj, gain, cos, sin):
    val = proj.astype(F32)
    scale = rms(val)
    unit = val * scale
    d_scaled = d_rot * cos - pltpu.roll(d_rot, 64, axis=1) * sin
    d_gain = jnp.sum(d_scaled * unit, axis=0, keepdims=True)
    return norm_backward(d_scaled * gain, unit, scale).astype(BF16), d_gain


def cols(i, width):
    return pl.ds(pl.multiple_of(i * width, width), width)


def spread_pair(i):
    return lax.div(i, 4), lax.rem(lax.div(i, 2), 2), lax.rem(i, 2)


def layer_kernel(
    x_ref, dy_ref, cos_ref, sin_ref, gq_ref, gk_ref, gains, wq, wk, wv, wo, wg, wu, wd,
    y_ref, dh_ref, oqkv, ogu, owo, owd, ogain,
    gbuf, bq, bk, bv, bo, bg, bu, bd, g1, g2,
    nt_ref, mt_ref, dres_ref, at_ref, ct_ref, dqkv_ref, dgu_ref, gpart_ref,
    nbuf, mbuf, dybuf, drbuf, gubuf, qkvbuf, abuf, cbuf, zgu, zqkv, zwd, zwo, gainbuf,
    link_send, link_recv, core_send, core_recv, local_sem, one_send, one_recv, one_local, far_send, far_recv,
):
    place = Place()
    me = place.me
    sems = (link_send, link_recv, core_send, core_recv, local_sem)
    one = (one_send, one_recv, one_local)
    count = [0]

    def part(src, buf, sub, order, axes=(Z, Y, X, C)):
        made = Spread(place, src, buf, sub, order, axes, sems, count[0])
        count[0] += 1
        return made

    rows_all = (ALL, ALL)
    gain_part = part(gains, gbuf, rows_all, ORDERS[0])
    p_q = part(wq, bq, rows_all, ORDERS[0])
    p_k = part(wk, bk, rows_all, ORDERS[1])
    p_v = part(wv, bv, rows_all, ORDERS[1])
    p_o = part(wo, bo, rows_all, ORDERS[2])
    early = [p_q, p_k, p_v, p_o]
    p_d = [part(wd, bd, (pl.ds(64 * i, 64), ALL), ORDERS[i]) for i in range(3)]
    p_g = [part(wg, bg, (ALL, pl.ds(1024 * i, 1024)), ORDERS[i]) for i in range(3)]
    p_u = [part(wu, bu, (ALL, pl.ds(1024 * i, 1024)), ORDERS[i]) for i in range(3)]
    late = p_d + p_g + p_u

    grp_gu, grp_qkv, grp_row = Group(place, Z), Group(place, Y), Group(place, X)

    def halves(src, buf, group):
        size = src.shape[0] // 2
        return [part(src, buf, (pl.ds(i * size, size), ALL), group.orders[i], group.axes) for i in range(2)]

    p_m = halves(mt_ref, mbuf, grp_gu)
    p_n = halves(nt_ref, nbuf, grp_qkv)
    p_dy = halves(dy_ref, dybuf, grp_row)
    p_dr = halves(dres_ref, drbuf, grp_row)

    def share(number, group, piece, buf):
        return Exchange(group, number, piece, buf.at[group.position], buf.at[pl.ds(0, 7)], one)

    def cols_for(group, ref, width):
        return lambda bit: ref.at[:, pl.ds(pl.multiple_of(group.spot(bit) * width, 128), width)]

    e_gu = share(0, grp_gu, cols_for(grp_gu, dgu_ref, 768), gubuf)
    e_qkv = share(1, grp_qkv, cols_for(grp_qkv, dqkv_ref, 512), qkvbuf)
    e_a = share(2, grp_row, lambda bit: at_ref.at[grp_row.across(bit)], abuf)
    e_c = share(3, grp_row, lambda bit: ct_ref.at[grp_row.across(bit)], cbuf)

    barrier = pltpu.get_barrier_semaphore()

    def other(k):
        return (lax.rem(me + k, 16),)

    def greet(k, _):
        pl.semaphore_signal(barrier, inc=1, device_id=other(k), device_id_type=MESH)
        return 0

    lax.fori_loop(1, 16, greet, 0)
    pl.semaphore_wait(barrier, 15)

    def gain_copy(k):
        return pltpu.make_async_remote_copy(
            src_ref=gpart_ref, dst_ref=gainbuf.at[me], send_sem=one_send.at[9], recv_sem=one_recv.at[9],
            device_id=other(k), device_id_type=MESH,
        )

    def far(group, number, source, target):
        return pltpu.make_async_remote_copy(
            src_ref=source, dst_ref=target, send_sem=far_send.at[number], recv_sem=far_recv.at[number],
            device_id=place.near(group.third), device_id_type=MESH,
        )

    for item in [gain_part] + early + late:
        item.begin()
    for item in [gain_part] + early:
        item.advance(0)
    for item in [gain_part] + early:
        item.advance(1)
    for item in late:
        item.advance(0)

    def local_pass(n_s, q_s, k_s, v_s, qr, kr, probs, ctx, h_s, m_s, gate, act, dact, dm, dres, dctx):
        gain_part.advance(2)
        gain_part.arrived()
        lane = lax.broadcasted_iota(jnp.int32, (8, 128), 1) < 64
        for i in range(8):
            first = gbuf[i // 4, (i // 2) % 2, i % 2, 0]
            second = gbuf[i // 4, (i // 2) % 2, i % 2, 1]
            g1[:, 128 * i : 128 * i + 128] = jnp.where(lane, first, pltpu.roll(second, 64, axis=1))[:1]
            g2[:, 128 * i : 128 * i + 128] = jnp.where(lane, pltpu.roll(first, 64, axis=1), second)[:1]

        def norm_rows(i, _):
            rows = cols(i, 32)
            val = x_ref[rows].astype(F32)
            n_s[rows] = (val * rms(val) * g1[...]).astype(BF16)
            return 0

        lax.fori_loop(0, 4, norm_rows, 0)

        def transpose_into(src, dst, blocks):
            def body(i, _):
                dst[cols(i, 128)] = src[:, cols(i, 128)].astype(F32).T.astype(BF16)
                return 0

            lax.fori_loop(0, blocks, body, 0)

        transpose_into(n_s, nt_ref, 8)

        for item in early:
            item.advance(2)

        def project(src, buf, dst, depth, width, tiles):
            def body(j, _):
                weight = buf[:, :, :, :, :, cols(j, width)].reshape(depth, width)
                dst[:, cols(j, width)] = nn(src[...], weight).astype(BF16)
                return 0

            lax.fori_loop(0, tiles, body, 0)

        p_q.arrived()
        project(n_s, bq, q_s, D, 512, 4)
        p_k.arrived()
        project(n_s, bk, k_s, D, 512, 2)
        p_v.arrived()
        project(n_s, bv, v_s, D, 512, 2)

        cos, sin = cos_ref, sin_ref
        scale = HD ** -0.5

        def attend(j, _):
            kv = cols(j, HD)
            pair = cols(j, 2 * HD)
            k_rot = head_forward(k_s[:, kv], gk_ref[...], cos[...], sin[...])
            kr[:, kv] = k_rot
            q_pair = q_s[:, pair]
            q_rot = jnp.concatenate(
                [head_forward(q_pair[:, HD * i : HD * i + HD], gq_ref[...], cos[...], sin[...]) for i in range(2)], axis=0
            )
            qr[j] = q_rot
            scores = nt(q_rot, k_rot) * scale
            row = lax.rem(lax.broadcasted_iota(jnp.int32, (2 * T, T), 0), T)
            col = lax.broadcasted_iota(jnp.int32, (2 * T, T), 1)
            scores = jnp.where(row >= col, scores, -1e30)
            expd = jnp.exp(scores - jnp.max(scores, axis=-1, keepdims=True))
            prob = expd / jnp.sum(expd, axis=-1, keepdims=True)
            probs[j] = prob
            out = nn(prob.astype(BF16), v_s[:, kv])
            ctx[:, pair] = jnp.concatenate([out[:T], out[T:]], axis=1).astype(BF16)
            return 0

        lax.fori_loop(0, 8, attend, 0)
        for item in late:
            item.advance(1)

        def ctx_turned(i, _):
            ct_ref[spread_pair(i)] = ctx[:, cols(i, 256)].astype(F32).T.astype(BF16).reshape(2, 128, T)
            return 0

        lax.fori_loop(0, 8, ctx_turned, 0)

        p_o.arrived()

        def out_proj(j, _):
            tile = cols(j, 256)
            weight = bo[:, :, :, :, :, tile].reshape(NQ, 256)
            attn = nn(ctx[...], weight).astype(BF16)
            h_s[:, tile] = (x_ref[:, tile].astype(F32) + attn.astype(F32)).astype(BF16).astype(F32)
            return 0

        lax.fori_loop(0, 4, out_proj, 0)

        def norm2_rows(i, _):
            rows = cols(i, 32)
            val = h_s[rows]
            m_s[rows] = (val * rms(val) * g2[...]).astype(BF16)
            return 0

        lax.fori_loop(0, 4, norm2_rows, 0)
        transpose_into(m_s, mt_ref, 8)
        for item in p_m + p_dy + p_n:
            item.begin()
        e_c.begin()

        for item in p_d:
            item.advance(2)
        for item in p_d:
            item.arrived()

        def d_act(i, _):
            weight = bd[lax.div(i, 4), lax.rem(lax.div(i, 2), 2), lax.rem(i, 2)].reshape(384, D)
            dact[:, cols(i, 384)] = nt(dy_ref[...], weight)
            return 0

        lax.fori_loop(0, 8, d_act, 0)
        for item in p_g:
            item.advance(2)
        for item in p_g:
            item.arrived()
        project(m_s, bg, gate, D, 512, 6)
        for item in p_u:
            item.advance(2)
        for item in p_u:
            item.arrived()

        def up_tile(j, _):
            tile = cols(j, 256)
            weight = bu[:, :, :, :, :, tile].reshape(D, 256)
            up_val = nn(m_s[...], weight).astype(BF16).astype(F32)
            gate_val = gate[:, tile].astype(F32)
            sig = jax.nn.sigmoid(gate_val)
            act_val = (gate_val * sig * up_val).astype(BF16)
            act[:, tile] = act_val
            d_act_val = dact[:, tile]
            d_gate = (d_act_val * up_val * sig * (1.0 + gate_val * (1.0 - sig))).astype(BF16)
            dgu_ref[:, tile] = d_gate
            dgu_ref[:, cols(j + FF // 256, 256)] = (d_act_val * gate_val * sig).astype(BF16)
            return 0

        lax.fori_loop(0, FF // 256, up_tile, 0)
        e_gu.begin()

        def act_turned(i, _):
            at_ref[spread_pair(i)] = act[:, cols(i, 384)].astype(F32).T.astype(BF16).reshape(2, 192, T)
            return 0

        lax.fori_loop(0, 8, act_turned, 0)
        for item in p_m + p_dy + p_n:
            item.advance(0)
        e_a.begin()

        def d_mlp_in(i, _):
            zi, yi = lax.div(i, 2), lax.rem(i, 2)
            grad = nt(dgu_ref[:, :FF], bg[zi, yi].reshape(256, FF))
            dm[:, cols(i, 256)] = grad + nt(dgu_ref[:, FF:], bu[zi, yi].reshape(256, FF))
            return 0

        lax.fori_loop(0, 4, d_mlp_in, 0)
        for item in p_m + p_dy + p_n:
            item.advance(1)

        def d_res_rows(i, total):
            rows = cols(i, 32)
            val = h_s[rows]
            r_scale = rms(val)
            unit = val * r_scale
            grad = dm[rows]
            out = dy_ref[rows].astype(F32) + norm_backward(grad * g2[...], unit, r_scale)
            dres[rows] = out
            dres_ref[rows] = out.astype(BF16)
            return total + jnp.sum(grad * unit, axis=0, keepdims=True)

        d_g2 = lax.fori_loop(0, 4, d_res_rows, jnp.zeros((1, D), F32))
        for i in range(8):
            gpart_ref[8 + i : 9 + i, :] = d_g2[:, 128 * i : 128 * i + 128]

        for item in p_dr:
            item.begin()

        def d_ctx(i, _):
            weight = bo[lax.div(i, 2), lax.rem(i, 2)].reshape(512, D)
            dctx[:, cols(i, 512)] = nt(dres_ref[...], weight).astype(BF16)
            return 0

        lax.fori_loop(0, 4, d_ctx, 0)
        for item in p_dr:
            item.advance(0)

        def attend_back(j, carry):
            q_total, k_total = carry
            kv = cols(j, HD)
            pair = cols(j, 2 * HD)
            d_out = dctx[:, pair]
            d_out = jnp.concatenate([d_out[:, :HD], d_out[:, HD:]], axis=0)
            prob = probs[j]
            d_value = tn(prob.astype(BF16), d_out).astype(BF16)
            d_prob = nt(d_out, v_s[:, kv])
            d_score = prob * (d_prob - jnp.sum(prob * d_prob, axis=-1, keepdims=True))
            d_score = (d_score * scale).astype(BF16)
            d_q_rot = nn(d_score, kr[:, kv])
            d_k_rot = tn(d_score, qr[j])
            q_pair = q_s[:, pair]
            d_q0, g_q0 = head_backward(d_q_rot[:T], q_pair[:, :HD], gq_ref[...], cos[...], sin[...])
            d_q1, g_q1 = head_backward(d_q_rot[T:], q_pair[:, HD:], gq_ref[...], cos[...], sin[...])
            d_k, g_k = head_backward(d_k_rot, k_s[:, kv], gk_ref[...], cos[...], sin[...])
            dqkv_ref[:, pair] = jnp.concatenate([d_q0, d_q1], axis=1)
            dqkv_ref[:, cols(j + 16, HD)] = d_k
            dqkv_ref[:, cols(j + 24, HD)] = d_value
            return q_total + g_q0 + g_q1, k_total + g_k

        zero = jnp.zeros((1, HD), F32)
        q_total, k_total = lax.fori_loop(0, 8, attend_back, (zero, zero))
        e_qkv.begin()
        for item in p_dr:
            item.advance(1)
        gpart_ref[16:17, :] = q_total
        gpart_ref[17:18, :] = k_total
        gpart_ref[18:24, :] = jnp.zeros((6, 128), F32)

        def d_normed(i, _):
            zi, yi = lax.div(i, 2), lax.rem(i, 2)
            grad = nt(dqkv_ref[:, :NQ], bq[zi, yi].reshape(256, NQ))
            grad += nt(dqkv_ref[:, NQ : NQ + D], bk[zi, yi].reshape(256, D))
            dm[:, cols(i, 256)] = grad + nt(dqkv_ref[:, NQ + D :], bv[zi, yi].reshape(256, D))
            return 0

        lax.fori_loop(0, 4, d_normed, 0)

        def d_hidden_rows(i, total):
            rows = cols(i, 32)
            val = x_ref[rows].astype(F32)
            x_scale = rms(val)
            unit = val * x_scale
            grad = dm[rows]
            dh_ref[rows] = (dres[rows] + norm_backward(grad * g1[...], unit, x_scale)).astype(BF16)
            return total + jnp.sum(grad * unit, axis=0, keepdims=True)

        d_g1 = lax.fori_loop(0, 4, d_hidden_rows, jnp.zeros((1, D), F32))
        for i in range(8):
            gpart_ref[i : i + 1, :] = d_g1[:, 128 * i : 128 * i + 128]

        def gain_send(k, _):
            gain_copy(k).start()
            return 0

        lax.fori_loop(1, 16, gain_send, 0)

        def down(j, _):
            tile = cols(j, 256)
            weight = bd[:, :, :, :, :, tile].reshape(FF, 256)
            out = nn(act[...], weight).astype(BF16).astype(F32)
            y_ref[:, tile] = (h_s[:, tile] + out).astype(BF16)
            return 0

        lax.fori_loop(0, 4, down, 0)

    pl.run_scoped(
        local_pass,
        VM((T, D), BF16), VM((T, NQ), BF16), VM((T, D), BF16), VM((T, D), BF16),
        VM((8, 2 * T, HD), BF16), VM((T, D), BF16), VM((8, 2 * T, T), F32), VM((T, NQ), BF16), VM((T, D), F32),
        VM((T, D), BF16), VM((T, FF), BF16), VM((T, FF), BF16), VM((T, FF), F32),
        VM((T, D), F32), VM((T, D), F32), VM((T, NQ), BF16),
    )

    inv_tokens = 1.0 / (16 * T)

    def lanes(buf, rows):
        blocks = [buf[i // 4, (i // 2) % 2, i % 2, rows] for i in range(8)]
        return jnp.concatenate(blocks, axis=1)

    def gradients(rgu, rqkv, rwd, rwo):
        def column_chunk(acts, grads, out, chunk):
            def tile(i, _):
                right = grads[:, :, 256 * chunk : 256 * chunk + 256].reshape(8 * T, 256)
                block = nn(lanes(acts, cols(i, 128)), right) * inv_tokens
                out[(chunk,) + spread_pair(i)] = block.reshape(2, 64, 256)
                return 0

            lax.fori_loop(0, 8, tile, 0)

        def send_chunk(group, result, target, chunk, number):
            return far(group, number, result.at[(chunk,) + group.side(False)], target.at[chunk])

        for item in p_m:
            item.arrived()
        e_gu.arrived()
        gu_far = [send_chunk(grp_gu, rgu, zgu, chunk, chunk) for chunk in range(3)]
        for chunk in range(3):
            column_chunk(mbuf, gubuf, rgu, chunk)
            gu_far[chunk].start()

        for item in p_dy:
            item.arrived()
        e_a.arrived()
        e_c.arrived()

        def row_tile(left_buf, right_buf, out, height):
            def body(j, _):
                tile = cols(lax.rem(j, 4), 256)
                half = lax.div(j, 4)
                left = jnp.concatenate([left_buf[i, half] for i in range(8)], axis=1)
                right = right_buf[:, :, :, :, tile].reshape(8 * T, 256)
                out[half, :, tile] = nn(left, right) * inv_tokens
                return 0

            lax.fori_loop(0, 8, body, 0)

        side = place.bit[X]
        row_tile(abuf, dybuf, rwd, 192)
        wd_far = far(grp_row, 5, rwd.at[1 - side], zwd)
        wd_far.start()

        for item in p_n:
            item.arrived()
        e_qkv.arrived()
        qkv_far = [send_chunk(grp_qkv, rqkv, zqkv, chunk, 3 + chunk) for chunk in range(2)]
        for chunk in range(2):
            column_chunk(nbuf, qkvbuf, rqkv, chunk)
            qkv_far[chunk].start()

        for item in p_dr:
            item.arrived()
        row_tile(cbuf, drbuf, rwo, 128)
        wo_far = far(grp_row, 6, rwo.at[1 - side], zwo)
        wo_far.start()

        def final(group, number, result, target, out, chunk, width):
            for bit in group.members():
                index = (chunk,) + tuple(bit)
                result[index] = result[index] + target[(chunk,) + tuple(bit[dim] for dim in group.axes)]
            where = pl.ds(pl.multiple_of(group.position * width + 256 * chunk, 128), 256)
            move = Exchange(
                group, number, lambda bit: result.at[(chunk,) + tuple(bit)], out.at[:, where],
                out.at[:, pl.ds(0, 7 * 256)], one,
            )
            move.begin()
            return move

        moves = []
        for kind, chunk in ((0, 0), (1, 0), (0, 1), (1, 1), (0, 2)):
            if kind == 0:
                gu_far[chunk].wait_recv()
                moves.append(final(grp_gu, 4 + chunk, rgu, zgu, ogu, chunk, 768))
            else:
                qkv_far[chunk].wait_recv()
                moves.append(final(grp_qkv, 7 + chunk, rqkv, zqkv, oqkv, chunk, 512))
        wd_far.wait_recv()
        owd[...] = rwd[side] + zwd[...]
        wo_far.wait_recv()
        owo[...] = rwo[side] + zwo[...]

        pltpu.make_async_copy(gainbuf.at[pl.ds(0, 15)], gainbuf.at[pl.ds(0, 15)], one_recv.at[9]).wait()
        gainbuf[me] = gpart_ref[...]
        total = gainbuf[0]
        for i in range(1, 16):
            total = total + gainbuf[i]
        ogain[...] = total * inv_tokens
        for move in moves:
            move.arrived()
            move.drain()
        for copy in gu_far + qkv_far + [wd_far, wo_far]:
            copy.wait_send()

    pl.run_scoped(
        gradients,
        VM((3, 2, 2, 2, 2, 64, 256), F32), VM((2, 2, 2, 2, 2, 64, 256), F32), VM((2, 192, D), F32), VM((2, 128, D), F32),
    )
    pltpu.make_async_copy(gainbuf.at[pl.ds(0, 15)], gainbuf.at[pl.ds(0, 15)], one_send.at[9]).wait()
    for item in (e_gu, e_qkv, e_a, e_c):
        item.drain()
    for item in [gain_part] + early + late + p_m + p_n + p_dy + p_dr:
        item.drain()


def gather_sems(parts):
    dma = pltpu.SemaphoreType.DMA
    return [dma((parts, 3)), dma((parts, 3)), dma((parts, 4)), dma((parts, 4)), dma((parts,))]


def cube(rows, width, dtype):
    return VM((2, 2, 2, 2, rows, width), dtype)


def square(rows, width):
    return VM((2, 2, 2, rows, width), BF16)


def shape(rows, width, dtype):
    return jax.ShapeDtypeStruct((rows, width), dtype)


def layer_call(x, dy, cos, sin, gq, gk, gains, *weights):
    vmem = pl.BlockSpec(memory_space=VM)
    hbm = pl.BlockSpec(memory_space=pl.ANY)
    dma = pltpu.SemaphoreType.DMA
    return pl.pallas_call(
        layer_kernel,
        name="layer",
        out_shape=(
            shape(T, D, BF16), shape(T, D, BF16), shape(64, NQ + 2 * D, F32), shape(64, 2 * FF, F32),
            shape(128, D, F32), shape(192, D, F32), shape(24, 128, F32),
        ),
        in_specs=[vmem] * 6 + [hbm] * 8,
        out_specs=(vmem, vmem, hbm, hbm, vmem, vmem, vmem),
        scratch_shapes=[
            cube(8, 128, F32), cube(64, NQ, BF16), cube(64, D, BF16), cube(64, D, BF16), cube(128, D, BF16),
            cube(64, FF, BF16), cube(64, FF, BF16), cube(192, D, BF16), VM((1, D), F32), VM((1, D), F32),
            VM((D, T), BF16), VM((D, T), BF16), VM((T, D), BF16), cube(192, T, BF16), cube(128, T, BF16),
            VM((T, NQ + 2 * D), BF16), VM((T, 2 * FF), BF16), VM((24, 128), F32),
            square(D, T), square(D, T), square(T, D), square(T, D),
            VM((8, T, 768), BF16), VM((8, T, 512), BF16), VM((8, 2, 192, T), BF16), VM((8, 2, 128, T), BF16),
            VM((3, 2, 2, 2, 64, 256), F32), VM((2, 2, 2, 2, 64, 256), F32), VM((192, D), F32), VM((128, D), F32),
            VM((16, 24, 128), F32),
        ] + gather_sems(22) + [dma((10,)), dma((10,)), dma((10,)), dma((7,)), dma((7,))],
        compiler_params=pltpu.CompilerParams(collective_id=0, has_side_effects=True, vmem_limit_bytes=HIGH_VMEM),
    )(x, dy, cos, sin, gq, gk, gains, *weights)


def rope_tables(positions):
    inv_freq = ROPE_THETA ** (-2.0 * jnp.arange(HD // 2, dtype=F32) / HD)
    angle = positions.reshape(-1, 1).astype(F32) * inv_freq
    cos_half, sin_half = jnp.cos(angle), jnp.sin(angle)
    return jnp.concatenate([cos_half, cos_half], axis=-1), jnp.concatenate([-sin_half, sin_half], axis=-1)


def solution(mesh):
    axis_name = mesh.axis_names[0]
    sharded = P(axis_name)
    in_specs = (sharded,) * 5 + (P(), P()) + (sharded,) * 7
    out_specs = (sharded,) * 4 + (P(), P()) + (sharded,) * 7

    def device_step(hidden, grad_out, positions, norm1, norm2, gain_q, gain_k, w_q, w_k, w_v, w_o, w_gate, w_up, w_down):
        cos, sin = rope_tables(positions)
        gains = jnp.broadcast_to(jnp.concatenate([norm1, norm2]).astype(F32)[None, :], (8, 128))
        x, dy = hidden.reshape(T, D), grad_out.reshape(T, D)
        gq, gk = gain_q.astype(F32)[None, :], gain_k.astype(F32)[None, :]
        out, d_hidden, d_qkv, d_gate_up, d_wo, d_wd, g_sum = layer_call(
            x, dy, cos, sin, gq, gk, gains, w_q, w_k, w_v, w_o, w_gate, w_up, w_down
        )
        start = lax.axis_index(axis_name) * 64
        d_norm1 = lax.dynamic_slice(g_sum[:8].reshape(D), (start,), (64,))
        d_norm2 = lax.dynamic_slice(g_sum[8:16].reshape(D), (start,), (64,))
        return (
            out.reshape(hidden.shape), d_hidden.reshape(hidden.shape), d_norm1, d_norm2, g_sum[16], g_sum[17],
            d_qkv[:, :NQ], d_qkv[:, NQ : NQ + D], d_qkv[:, NQ + D :], d_wo, d_gate_up[:, :FF], d_gate_up[:, FF:], d_wd,
        )

    return jax.shard_map(device_step, mesh=mesh, in_specs=in_specs, out_specs=out_specs, check_vma=False)
```

time: 1170 us -> 256 us (0.22)
  waiting for transfers between devices: 885 us -> 0 us
  Pallas kernels: 0 us -> 240 us
  matrix products: 107 us -> 0 us
  blocking collectives: 99.2 us -> 0 us
  other arithmetic: 25.5 us -> 3.67 us
  local copies, waits for them, and re-layouts: 30.8 us -> 11.9 us
  between operations: 15.4 us -> 0.69 us
    reduce_scatter x7 -> x0, waiting for transfers between devices: 570 us -> none  [device_step(): lax.psum_scatter(row_grad * inv_tokens, axis_name, scatter_dimension=0, t...]
    all_gather x14 -> x0, waiting for transfers between devices: 307 us -> none  [gather_weights(): lax.all_gather(row_shard, axis_name, axis=0, tiled=True)]
    pallas_call x0 -> x1, Pallas kernels: none -> 240 us  [layer_call(): pl.pallas_call(layer_kernel, name='layer', out_shape=(shape(T, D, BF16),...]
    dot_general x26 -> x0, matrix products: 105 us -> none  [the longest x7 35.7 us: matmul_tn(): lax.dot_general(left_op, right_op, (((0,), (0,)), ((), ())), preferred_el...]
    unnamed x3 -> x0, blocking collectives: 99.2 us -> none
  transfers between devices with their start and end apart: 21 -> 0, of which waited for: 17 -> 0; matrix products, arithmetic and copies ran while one was open for 13% -> 0% of each run, Pallas kernels for 0% -> 0%
where the time goes in v1:
time: 256 us
  Pallas kernels  240 us (94%)
  local copies, waits for them, and re-layouts  11.9 us (5%)
  other arithmetic  3.67 us (1%)
    pallas_call x1, Pallas kernels, layer_call(): pl.pallas_call(layer_kernel, name='layer', out_shape=(shape(T, D, BF16),...  240 us

profile of v1, /device:TPU:0, one launch (start us, length us, event | category | flops | bytes accessed | tf_op | source)
XLA Modules:
  0.0 256.1 jit_solution(13559900540293445446)
XLA Ops:
  0.6 0.7 convert_bitcast_fusion
  1.3 0.7 maximum_convert_fusion
  2.1 1.2 bitcast_convert_fusion
  3.3 0.6 broadcast_in_dim.21.gains
  3.9 0.3 fusion
  4.2 0.8 pad_maximum_fusion
  4.9 239.9 %layer.1 = (bf16[128,1024]{1,0:T(8,128)(2,1)}, bf16[128,1024]{1,0:T(8,128)(2,1)}, f32[64,4096]{1,0:T(8,128)}, f32[64,6144]{1,0:T(8,128)}, f32[128,1024]{1,0:T(8,...) custom-call(bf16[128,1024]{1,0:T(8,128)(2,1)} %bitcast.20, bf16[128,1024]{1,0:T(8,128)(2,1)} %bitcast.21, ...), custom_call_target="tpu_custom_call" | custom-call | tf_op jit(solution)/shard_map/layer/pallas_call | solution.py:694
  244.9 0.0 copy-start
  244.9 1.3 slice_bitcast_fusion.2
  246.2 0.7 slice_bitcast_fusion
  246.9 0.6 dynamic_slice.7
  247.5 0.6 dynamic_slice.6
  248.0 1.9 slice.31
  249.9 1.9 fusion.2
  251.8 0.0 copy-done
  251.8 0.0 copy-start.4
  251.8 0.0 copy-start.3
  251.8 0.0 copy-start.2
  251.8 1.3 fusion.1
  253.1 0.0 copy-start.1
  253.1 0.0 copy-done.4
  253.1 0.7 copy.31
  253.8 0.0 copy-done.3
  253.8 0.7 copy.32
  254.5 0.0 copy-done.2
  254.5 0.8 copy.33
  255.3 0.0 copy-done.1
  255.3 0.9 copy.34
  (1 shorter events, 0.0 us)
Async XLA Ops:
  244.9 6.9 %copy-start = (f32[64,6144]{1,0:T(8,128)S(1)}, f32[64,6144]{1,0:T(8,128)}, u32[]{:S(2)}) copy-start(f32[64,6144]{1,0:T(8,128)} %get-tuple-element.25) | copy-start | bytes 4718596
  251.8 1.3 copy-start.4
  251.8 2.0 copy-start.3
  251.8 2.7 %copy-start.2 = (f32[128,1024]{1,0:T(8,128)S(1)}, f32[128,1024]{1,0:T(8,128)}, u32[]{:S(2)}) copy-start(f32[128,1024]{1,0:T(8,128)} %get-tuple-element.64) | copy-start | bytes 1572868
  253.1 2.2 copy-start.1

commit v2 on v0

v2 whole, which is shorter than its diff:
```python
import jax
import jax.numpy as jnp
from jax import lax
from jax.experimental import pallas as pl
from jax.experimental.pallas import tpu as pltpu
from jax.sharding import PartitionSpec as P

RMS_EPS = 1e-6
ROPE_THETA = 1000000.0
MESH = pl.DeviceIdType.MESH
F32 = jnp.float32
BF16 = jnp.bfloat16
T = 128
D = 1024
NQ = 2048
FF = 3072
HD = 128
Z, Y, X, C = 0, 1, 2, 3
STRIDE = (8, 4, 2, 1)
ALL = slice(None)
VM = pltpu.VMEM
HIGH_VMEM = 67043328


def nn(left_op, right_op):
    return jnp.dot(left_op, right_op, preferred_element_type=F32)


def nt(left_op, right_op):
    return lax.dot_general(left_op, right_op, (((1,), (1,)), ((), ())), preferred_element_type=F32)


def tn(left_op, right_op):
    return lax.dot_general(left_op, right_op, (((0,), (0,)), ((), ())), preferred_element_type=F32)


def rms(val):
    return lax.rsqrt(jnp.mean(val * val, axis=-1, keepdims=True) + RMS_EPS)


def norm_backward(d_unit, unit_val, scale_val):
    return scale_val * (d_unit - unit_val * jnp.mean(d_unit * unit_val, axis=-1, keepdims=True))


class Place:
    def __init__(self):
        self.me = lax.axis_index("fsdp")
        self.bit = [lax.rem(lax.div(self.me, s), 2) for s in STRIDE]

    def near(self, dim):
        return (self.me + STRIDE[dim] * (1 - 2 * self.bit[dim]),)

    def greet(self, dims):
        barrier = pltpu.get_barrier_semaphore()
        for dim in dims:
            pl.semaphore_signal(barrier, inc=1, device_id=self.near(dim), device_id_type=MESH)
        pl.semaphore_wait(barrier, len(dims))


class Spread:
    def __init__(self, place, own, first, buf, sub, order, axes, sems, part):
        self.place, self.buf, self.sub, self.order, self.axes = place, buf, sub, order, axes
        self.link_send, self.link_recv, self.core_send, self.core_recv, self.local_sem = sems
        self.part, self.last = part, len(order)
        self.source = own
        self.mine = self.block(()) if own is None else own
        self.first = self.mine if first is None else first

    def block(self, full, flip=None):
        index = []
        for dim in self.axes:
            if dim in full:
                index.append(ALL)
            elif dim == flip:
                index.append(1 - self.place.bit[dim])
            else:
                index.append(self.place.bit[dim])
        return self.buf.at[tuple(index) + self.sub]

    def copy_own(self):
        return pltpu.make_async_copy(self.source, self.block(()), self.local_sem.at[self.part])

    def link(self, step):
        dst = self.block(self.order[:step])
        return pltpu.make_async_remote_copy(
            src_ref=self.first if step == 0 else dst,
            dst_ref=dst,
            send_sem=self.link_send.at[self.part, step],
            recv_sem=self.link_recv.at[self.part, step],
            device_id=self.place.near(self.order[step]),
            device_id_type=MESH,
        )

    def core(self, step):
        dst = self.block(()) if step == 0 else self.block(self.order[: step - 1], self.order[step - 1])
        return pltpu.make_async_remote_copy(
            src_ref=self.mine if step == 0 else dst,
            dst_ref=dst,
            send_sem=self.core_send.at[self.part, step],
            recv_sem=self.core_recv.at[self.part, step],
            device_id=self.place.near(C),
            device_id_type=MESH,
        )

    def begin(self):
        self.link(0).start()
        if self.source is not None:
            self.copy_own().start()
        self.core(0).start()

    def advance(self, step):
        if step == 0 and self.source is not None:
            self.copy_own().wait()
        self.link(step).wait_recv()
        if step + 1 < self.last:
            self.link(step + 1).start()
        self.core(step + 1).start()

    def arrived(self):
        for step in range(self.last + 1):
            self.core(step).wait_recv()

    def drain(self):
        for step in range(self.last):
            self.link(step).wait_send()
        for step in range(self.last + 1):
            self.core(step).wait_send()


class Group:
    def __init__(self, place, axes):
        self.place, self.axes = place, axes
        self.position = self.spot(place.bit)

    def others(self):
        for number in range(2 ** len(self.axes) - 1, 0, -1):
            bit = list(self.place.bit)
            for i, dim in enumerate(self.axes):
                if number >> i & 1:
                    bit[dim] = 1 - bit[dim]
            yield bit

    def spot(self, bit):
        total = 0
        for dim in self.axes:
            total = total * 2 + bit[dim]
        return total


def device_of(bit):
    return (sum(stride * value for stride, value in zip(STRIDE, bit)),)


class Exchange:
    def __init__(self, group, number, piece, slot, blocks, sems):
        self.group, self.piece, self.slot, self.blocks = group, piece, slot, blocks
        self.send, self.recv, self.local = (sem.at[number] for sem in sems)

    def own(self):
        return pltpu.make_async_copy(self.piece(self.group.place.bit), self.slot, self.local)

    def begin(self):
        for bit in self.group.others():
            pltpu.make_async_remote_copy(
                src_ref=self.piece(bit),
                dst_ref=self.slot,
                send_sem=self.send,
                recv_sem=self.recv,
                device_id=device_of(bit),
                device_id_type=MESH,
            ).start()
        self.own().start()

    def arrived(self):
        self.own().wait()
        pltpu.make_async_copy(self.blocks, self.blocks, self.recv).wait()

    def drain(self):
        pltpu.make_async_copy(self.blocks, self.blocks, self.send).wait()


def head_forward(proj, gain, cos, sin):
    val = proj.astype(F32)
    scaled = val * rms(val) * gain
    return (scaled * cos + pltpu.roll(scaled, 64, axis=1) * sin).astype(BF16)


def head_backward(d_rot, proj, gain, cos, sin):
    val = proj.astype(F32)
    scale = rms(val)
    unit = val * scale
    d_scaled = d_rot * cos - pltpu.roll(d_rot, 64, axis=1) * sin
    d_gain = jnp.sum(d_scaled * unit, axis=0, keepdims=True)
    return norm_backward(d_scaled * gain, unit, scale).astype(BF16), d_gain


def cols(i, width):
    return pl.ds(pl.multiple_of(i * width, width), width)


def loop(count, body, init=0):
    return lax.fori_loop(0, count, body, init)


def each(count):
    def run(body):
        def step(i, _):
            body(i)
            return 0

        loop(count, step)

    return run


def two(i):
    return lax.div(i, 2), lax.rem(i, 2)


def three(i):
    return two(lax.div(i, 2)) + (lax.rem(i, 2),)


def layer_kernel(
    x_ref, dy_ref, trig_ref, gq_ref, gk_ref, gains, wq, wk, wv, wo, wg, wu, wd,
    y_ref, dh_ref, oqkv, ogu, owo, owd, ogain,
    gbuf, bq, bk, bv, bo, bg, bu, bd, g1, g2,
    xp, trig, n_s, q_s, k_s, v_s, qr, kr, probs, ctx, h_s, m_s, spare, act, dact, dctx, dres,
    part_a, part_y, part_m, part_n, land_a, land_y, land_m, land_n,
    at_ref, ct_ref, dqkv, dgu, gpart,
    nbuf, mbuf, dybuf, drbuf, gubuf, qkvbuf, abuf, cbuf,
    rgu, rqkv, rwd, rwo, zgu, zqkv, zwd, zwo, gainbuf,
    link_send, link_recv, core_send, core_recv, local_sem, one_send, one_recv, one_local, far_send, far_recv,
):
    place = Place()
    me = place.me
    z, y, x, c = place.bit
    sems = (link_send, link_recv, core_send, core_recv, local_sem)
    one = (one_send, one_recv, one_local)
    parts = []

    def spread(own, first, buf, sub, order, axes):
        parts.append(Spread(place, own, first, buf, sub, order, axes, sems, len(parts)))
        return parts[-1]

    both = (ALL, ALL)
    turns = ((Y, X), (X, Y))

    def by_columns(src, buf):
        half = src.shape[1] // 2
        size = half // 2
        made = []
        for i in range(2):
            mine, theirs = (src.at[:, pl.ds(pl.multiple_of(side * half + i * size, size), size)] for side in (z, 1 - z))
            made.append(spread(mine, theirs, buf, (ALL, pl.ds(i * size, size)), (Z,) + turns[i], (Z, Y, X, C)))
        return made

    def by_rows(src, buf):
        size = src.shape[0] // 2
        made = []
        for i in range(2):
            rows = pl.ds(i * size, size)
            made.append(spread(src.at[rows], None, buf, (rows, ALL), turns[i], (Y, X, C)))
        return made

    gain_part = spread(gains, None, gbuf, both, (X, Y, Z), (Z, Y, X, C))
    p_qkv = by_columns(wq, bq) + by_columns(wk, bk) + by_columns(wv, bv)
    p_o, p_d = by_rows(wo, bo), by_rows(wd, bd)
    p_g, p_u = by_columns(wg, bg), by_columns(wu, bu)
    p_m = spread(None, None, mbuf, both, (X,), (X, C))
    p_n = spread(None, None, nbuf, both, (Y,), (Y, C))
    p_dy = spread(None, None, dybuf, (ALL, ALL, ALL), (Y,), (Y, C))
    p_dr = spread(None, None, drbuf, (ALL, ALL, ALL), (X,), (X, C))

    grp_x, grp_y = Group(place, (X, C)), Group(place, (Y, C))

    def share(number, group, piece, buf):
        return Exchange(group, number, piece, buf.at[group.position], buf.at[pl.ds(0, 3)], one)

    def cols_for(group, ref, width):
        return lambda bit: ref.at[:, pl.ds(pl.multiple_of(group.spot(bit) * width, 128), width)]

    e_gu = share(0, grp_x, cols_for(grp_x, dgu, 768), gubuf)
    e_qkv = share(1, grp_y, cols_for(grp_y, dqkv, 512), qkvbuf)
    e_a = share(2, grp_y, lambda bit: at_ref.at[bit[Y], :, bit[C]], abuf)
    e_c = share(3, grp_x, lambda bit: ct_ref.at[:, bit[X], bit[C]], cbuf)
    gain_number = 9
    sent = []

    def near_copy(dim, source, target):
        number = len(sent)
        sent.append(
            pltpu.make_async_remote_copy(
                src_ref=source, dst_ref=target, send_sem=far_send.at[number], recv_sem=far_recv.at[number],
                device_id=place.near(dim), device_id_type=MESH,
            )
        )
        return sent[-1]

    mine, theirs = cols(z, T), cols(1 - z, T)
    barrier = pltpu.get_barrier_semaphore()

    def other(k):
        return (lax.rem(me + k, 16),)

    @each(15)
    def _(k):
        pl.semaphore_signal(barrier, inc=1, device_id=other(k + 1), device_id_type=MESH)

    pl.semaphore_wait(barrier, 15)

    def gain_copy(k):
        return pltpu.make_async_remote_copy(
            src_ref=gpart, dst_ref=gainbuf.at[me], send_sem=one_send.at[gain_number],
            recv_sem=one_recv.at[gain_number], device_id=other(k), device_id_type=MESH,
        )

    gain_part.begin()
    for item in p_qkv + p_o:
        item.begin()
    x_copy = near_copy(Z, x_ref, xp.at[mine])
    trig_copy = near_copy(Z, trig_ref, trig.at[z])
    x_copy.start()
    trig_copy.start()
    xp[mine] = x_ref[...]
    trig[z] = trig_ref[...]
    for step in range(3):
        gain_part.advance(step)
    for item in p_o + p_qkv:
        item.advance(0)
    for item in p_g + p_u:
        item.begin()
    dy_copy = near_copy(Z, dy_ref, dybuf.at[y, c, z])
    dy_copy.start()
    dybuf[y, c, z] = dy_ref[...]
    gain_part.arrived()
    lane = lax.broadcasted_iota(jnp.int32, (8, 128), 1) < 64
    for i in range(8):
        first, second = gbuf[i // 4, (i // 2) % 2, i % 2, 0], gbuf[i // 4, (i // 2) % 2, i % 2, 1]
        tile = slice(128 * i, 128 * i + 128)
        g1[:, tile] = jnp.where(lane, first, pltpu.roll(second, 64, axis=1))[:1]
        g2[:, tile] = jnp.where(lane, pltpu.roll(first, 64, axis=1), second)[:1]
    for item in p_qkv:
        item.advance(1)
    x_copy.wait_recv()

    @each(8)
    def _(i):
        rows = cols(i, 32)
        val = xp[rows].astype(F32)
        n_s[rows] = (val * rms(val) * g1[...]).astype(BF16)

    def turned(val):
        return val.astype(F32).T.astype(BF16)

    for item in p_o:
        item.advance(1)
    for item in p_d:
        item.begin()

    @each(4)
    def _(i):
        nbuf[y, c, cols(i, 256)] = turned(n_s[:, cols(i, 256)])

    for item in p_qkv:
        item.advance(2)
    for item in p_d + p_g + p_u:
        item.advance(0)
    trig_copy.wait_recv()

    def weight(buf, tile):
        block = buf[(ALL,) * (len(buf.shape) - 1) + (tile,)]
        return block.reshape(-1, block.shape[-1])

    def project(buf, dst, width, tiles):
        @each(tiles)
        def _(j):
            tile = cols(j, width)
            dst[:, tile] = nn(n_s[...], weight(buf, tile)).astype(BF16)

    for item in p_qkv:
        item.arrived()
    project(bq, q_s, 512, 2)
    project(bk, k_s, 512, 1)
    project(bv, v_s, 512, 1)
    scale = HD ** -0.5

    def sequence_head(j):
        seq, head = lax.div(j, 4), lax.rem(j, 4)
        return seq, head, cols(seq, T), cols(head, HD), cols(head, 2 * HD)

    @each(8)
    def _(j):
        seq, _, rows, kv, pair = sequence_head(j)
        cos, sin = trig[seq, :, :HD], trig[seq, :, HD:]
        k_rot = head_forward(k_s[rows, kv], gk_ref[...], cos, sin)
        kr[rows, kv] = k_rot
        q_pair = q_s[rows, pair]
        q_rot = jnp.concatenate(
            [head_forward(half, gq_ref[...], cos, sin) for half in (q_pair[:, :HD], q_pair[:, HD:])], axis=0
        )
        qr[j] = q_rot
        scores = nt(q_rot, k_rot) * scale
        row = lax.rem(lax.broadcasted_iota(jnp.int32, (2 * T, T), 0), T)
        col = lax.broadcasted_iota(jnp.int32, (2 * T, T), 1)
        scores = jnp.where(row >= col, scores, -1e30)
        expd = jnp.exp(scores - jnp.max(scores, axis=-1, keepdims=True))
        prob = expd / jnp.sum(expd, axis=-1, keepdims=True)
        probs[j] = prob
        out = nn(prob.astype(BF16), v_s[rows, kv])
        ctx[rows, pair] = jnp.concatenate([out[:T], out[T:]], axis=1).astype(BF16)

    def pair_sum(partial, landing, compute):
        copies = []
        for half in range(2):
            @each(2)
            def _(j):
                i = j + 2 * half
                partial[:, :, cols(i, 256)] = compute(i).reshape(2, T, 256)

            span = (ALL, pl.ds(512 * half, 512))
            copies.append(near_copy(Z, partial.at[(1 - z,) + span], landing.at[span]))
            copies[-1].start()
        return copies

    def received(copies):
        for copy in copies:
            copy.wait_recv()

    for item in p_o:
        item.arrived()
    a_copies = pair_sum(part_a, land_a, lambda i: nn(ctx[...], weight(bo, cols(i, 256))))
    for item in p_g + p_u:
        item.advance(1)
    for item in p_d:
        item.advance(1)

    @each(4)
    def _(i):
        ct_ref[two(i)] = turned(ctx[:, cols(i, 256)]).reshape(2, 128, 2 * T)

    received(a_copies)

    @each(4)
    def _(i):
        rows = cols(i, 32)
        attn = (part_a[z, rows] + land_a[rows]).astype(BF16)
        val = (x_ref[rows].astype(F32) + attn.astype(F32)).astype(BF16).astype(F32)
        h_s[rows] = val
        m_s[pl.ds(pl.multiple_of(z * T + i * 32, 32), 32)] = (val * rms(val) * g2[...]).astype(BF16)

    m_copy = near_copy(Z, m_s.at[mine], m_s.at[mine])
    m_copy.start()
    for item in p_d:
        item.arrived()
    dy_copy.wait_recv()

    @each(4)
    def _(i):
        dact[:, cols(i, 384)] = nt(dybuf[y, c].reshape(2 * T, D), bd[two(i)].reshape(384, D))

    for item in p_g + p_u:
        item.advance(2)
    m_copy.wait_recv()
    for item in p_g + p_u:
        item.arrived()
    fh = FF // 2

    @each(fh // 256)
    def _(j):
        tile = cols(j, 256)
        gate_val = nn(m_s[...], weight(bg, tile)).astype(BF16).astype(F32)
        up_val = nn(m_s[...], weight(bu, tile)).astype(BF16).astype(F32)
        sig = jax.nn.sigmoid(gate_val)
        act[:, tile] = (gate_val * sig * up_val).astype(BF16)
        d_act = dact[:, tile]
        dgu[:, tile] = (d_act * up_val * sig * (1.0 + gate_val * (1.0 - sig))).astype(BF16)
        dgu[:, cols(j + fh // 256, 256)] = (d_act * gate_val * sig).astype(BF16)

    def d_mlp_in(i):
        rows = two(i)
        return nt(dgu[:, :fh], bg[rows].reshape(256, fh)) + nt(dgu[:, fh:], bu[rows].reshape(256, fh))

    m_copies = pair_sum(part_m, land_m, d_mlp_in)
    e_gu.begin()

    @each(4)
    def _(i):
        mbuf[x, c, cols(i, 256)] = turned(m_s[:, cols(i, 256)])

    p_m.begin()
    p_n.begin()
    p_dy.begin()

    @each(4)
    def _(i):
        at_ref[two(i)] = turned(act[:, cols(i, 384)]).reshape(2, 192, 2 * T)

    e_a.begin()
    e_c.begin()
    received(m_copies)

    def d_res_rows(i, total):
        rows = cols(i, 32)
        val = h_s[rows]
        r_scale = rms(val)
        unit = val * r_scale
        grad = part_m[z, rows] + land_m[rows]
        out = dy_ref[rows].astype(F32) + norm_backward(grad * g2[...], unit, r_scale)
        dres[rows] = out
        drbuf[x, c, z, rows] = out.astype(BF16)
        return total + jnp.sum(grad * unit, axis=0, keepdims=True)

    d_g2 = loop(4, d_res_rows, jnp.zeros((1, D), F32))
    r_copy = near_copy(Z, drbuf.at[x, c, z], drbuf.at[x, c, z])
    r_copy.start()
    y_copies = pair_sum(part_y, land_y, lambda i: nn(act[...], weight(bd, cols(i, 256))))
    r_copy.wait_recv()
    p_dr.begin()

    @each(2)
    def _(i):
        dctx[:, cols(i, 512)] = nt(drbuf[x, c].reshape(2 * T, D), bo[i].reshape(512, D)).astype(BF16)

    def attend_back(j, carry):
        q_total, k_total = carry
        seq, head, rows, kv, pair = sequence_head(j)
        cos, sin = trig[seq, :, :HD], trig[seq, :, HD:]
        d_out = dctx[rows, pair]
        d_out = jnp.concatenate([d_out[:, :HD], d_out[:, HD:]], axis=0)
        prob = probs[j]
        d_value = tn(prob.astype(BF16), d_out).astype(BF16)
        d_prob = nt(d_out, v_s[rows, kv])
        d_score = prob * (d_prob - jnp.sum(prob * d_prob, axis=-1, keepdims=True))
        d_score = (d_score * scale).astype(BF16)
        d_q_rot = nn(d_score, kr[rows, kv])
        d_k_rot = tn(d_score, qr[j])
        q_pair = q_s[rows, pair]
        d_q0, g_q0 = head_backward(d_q_rot[:T], q_pair[:, :HD], gq_ref[...], cos, sin)
        d_q1, g_q1 = head_backward(d_q_rot[T:], q_pair[:, HD:], gq_ref[...], cos, sin)
        d_k, g_k = head_backward(d_k_rot, k_s[rows, kv], gk_ref[...], cos, sin)
        dqkv[rows, pair] = jnp.concatenate([d_q0, d_q1], axis=1)
        dqkv[rows, cols(head + 8, HD)] = d_k
        dqkv[rows, cols(head + 12, HD)] = d_value
        return q_total + g_q0 + g_q1, k_total + g_k

    zero = jnp.zeros((1, HD), F32)
    q_total, k_total = loop(8, attend_back, (zero, zero))
    e_qkv.begin()

    def d_normed(i):
        rows = two(i)
        grad = nt(dqkv[:, :D], bq[rows].reshape(256, D)) + nt(dqkv[:, D : D + 512], bk[rows].reshape(256, 512))
        return grad + nt(dqkv[:, D + 512 :], bv[rows].reshape(256, 512))

    n_copies = pair_sum(part_n, land_n, d_normed)
    inv_tokens = 1.0 / (16 * T)

    def column_chunk(acts, grads, out, chunk):
        @each(8)
        def _(i):
            rows = cols(i, 128)
            left = jnp.concatenate([acts[k // 2, k % 2, rows] for k in range(4)], axis=1)
            right = grads[:, :, 256 * chunk : 256 * chunk + 256].reshape(8 * T, 256)
            out[(chunk,) + three(i)] = (nn(left, right) * inv_tokens).reshape(2, 64, 256)

    def half_of(dim, result, chunk):
        bit = place.bit[dim]
        return result.at[(chunk,) + tuple(1 - bit if k == dim else ALL for k in range(4))]

    def row_tiles(left_buf, right_buf, out):
        @each(8)
        def _(j):
            tile = cols(lax.rem(j, 4), 256)
            half = lax.div(j, 4)
            left = jnp.concatenate([left_buf[i, half] for i in range(4)], axis=1)
            out[half, :, tile] = nn(left, weight(right_buf, tile)) * inv_tokens

    p_m.advance(0)
    p_n.advance(0)
    p_dy.advance(0)
    p_dr.advance(0)
    p_m.arrived()
    e_gu.arrived()
    gu_far = []
    for chunk in range(3):
        column_chunk(mbuf, gubuf, rgu, chunk)
        gu_far.append(near_copy(Y, half_of(Y, rgu, chunk), zgu.at[chunk]))
        gu_far[-1].start()
    p_n.arrived()
    e_qkv.arrived()
    qkv_far = []
    for chunk in range(2):
        column_chunk(nbuf, qkvbuf, rqkv, chunk)
        qkv_far.append(near_copy(X, half_of(X, rqkv, chunk), zqkv.at[chunk]))
        qkv_far[-1].start()
    p_dy.arrived()
    e_a.arrived()
    row_tiles(abuf, dybuf, rwd)
    wd_far = near_copy(X, rwd.at[1 - x], zwd)
    wd_far.start()
    p_dr.arrived()
    e_c.arrived()
    row_tiles(cbuf, drbuf, rwo)
    wo_far = near_copy(Y, rwo.at[1 - y], zwo)
    wo_far.start()

    received(n_copies)

    def d_hidden_rows(i, total):
        rows = cols(i, 32)
        val = x_ref[rows].astype(F32)
        x_scale = rms(val)
        unit = val * x_scale
        grad = part_n[z, rows] + land_n[rows]
        dh_ref[rows] = (dres[rows] + norm_backward(grad * g1[...], unit, x_scale)).astype(BF16)
        return total + jnp.sum(grad * unit, axis=0, keepdims=True)

    d_g1 = loop(4, d_hidden_rows, jnp.zeros((1, D), F32))
    for i in range(8):
        tile = slice(128 * i, 128 * i + 128)
        gpart[i : i + 1, :] = d_g1[:, tile]
        gpart[8 + i : 9 + i, :] = d_g2[:, tile]
    gpart[16:17, :] = q_total
    gpart[17:18, :] = k_total
    gpart[18:24, :] = jnp.zeros((6, 128), F32)

    @each(15)
    def _(k):
        gain_copy(k + 1).start()

    received(y_copies)

    @each(4)
    def _(i):
        rows = cols(i, 32)
        out = (part_y[z, rows] + land_y[rows]).astype(BF16).astype(F32)
        y_ref[rows] = (h_s[rows] + out).astype(BF16)

    def final(dim, number, result, target, out, chunk, base):
        group = Group(place, tuple(k for k in range(4) if k != dim))
        for bit in list(group.others()) + [place.bit]:
            index = (chunk,) + tuple(bit)
            result[index] = result[index] + target[(chunk,) + tuple(bit[k] for k in group.axes)]
        where = pl.ds(pl.multiple_of(base + 256 * chunk, 128), 256)
        move = Exchange(
            group, number, lambda bit: result.at[(chunk,) + tuple(bit)], out.at[:, where],
            out.at[:, pl.ds(0, 7 * 256)], one,
        )
        move.begin()
        return move

    gu_base = x * FF + z * fh + c * 768
    qkv_base = (1 - y) * (z * D + c * 512) + y * (NQ + c * D + z * 512)
    moves = []
    for kind, chunk in ((0, 0), (1, 0), (0, 1), (1, 1), (0, 2)):
        if kind == 0:
            gu_far[chunk].wait_recv()
            moves.append(final(Y, 4 + chunk, rgu, zgu, ogu, chunk, gu_base))
        else:
            qkv_far[chunk].wait_recv()
            moves.append(final(X, 7 + chunk, rqkv, zqkv, oqkv, chunk, qkv_base))
    wd_far.wait_recv()
    owd[...] = rwd[x] + zwd[...]
    wo_far.wait_recv()
    owo[...] = rwo[y] + zwo[...]
    fifteen = gainbuf.at[pl.ds(0, 15)]
    pltpu.make_async_copy(fifteen, fifteen, one_recv.at[gain_number]).wait()
    gainbuf[me] = gpart[...]
    ogain[...] = loop(16, lambda i, total: total + gainbuf[i], jnp.zeros((24, 128), F32)) * inv_tokens
    for move in moves:
        move.arrived()
    for item in moves + [e_gu, e_qkv, e_a, e_c] + parts:
        item.drain()
    for copy in sent:
        copy.wait_send()
    pltpu.make_async_copy(fifteen, fifteen, one_send.at[gain_number]).wait()


def shape(rows, width, dtype):
    return jax.ShapeDtypeStruct((rows, width), dtype)


def many(count, *args):
    return [VM(*args)] * count


def layer_call(x, dy, trig, gq, gk, gains, *weights):
    vmem = pl.BlockSpec(memory_space=VM)
    hbm = pl.BlockSpec(memory_space=pl.ANY)
    dma = pltpu.SemaphoreType.DMA
    t2, kvh, fh = 2 * T, D // 2, FF // 2
    cube, square, line = (2, 2, 2, 2), (2, 2, 2), (2, 2)
    spreads = 19
    return pl.pallas_call(
        layer_kernel,
        name="layer",
        out_shape=(
            shape(T, D, BF16), shape(T, D, BF16), shape(64, NQ + 2 * D, F32), shape(64, 2 * FF, F32),
            shape(128, D, F32), shape(192, D, F32), shape(24, 128, F32),
        ),
        in_specs=[vmem] * 5 + [hbm] * 8,
        out_specs=(vmem, vmem, hbm, hbm, vmem, vmem, vmem),
        scratch_shapes=[
            VM(cube + (8, 128), F32), VM(cube + (64, D), BF16), *many(2, cube + (64, kvh), BF16),
            VM(square + (128, D), BF16), *many(2, cube + (64, fh), BF16), VM(square + (192, D), BF16),
            *many(2, (1, D), F32),
            VM((t2, D), BF16), VM((2, T, t2), F32), VM((t2, D), BF16), VM((t2, D), BF16), *many(2, (t2, kvh), BF16),
            VM((8, t2, HD), BF16), VM((t2, kvh), BF16), VM((8, t2, T), F32), VM((t2, D), BF16), VM((T, D), F32),
            VM((t2, D), BF16), VM((8, 128), BF16), VM((t2, fh), BF16), VM((t2, fh), F32), VM((t2, D), BF16),
            VM((T, D), F32), *many(4, (2, T, D), F32), *many(4, (T, D), F32),
            VM(square + (192, t2), BF16), VM(square + (128, t2), BF16), VM((t2, NQ), BF16), VM((t2, FF), BF16),
            VM((24, 128), F32), *many(2, line + (D, t2), BF16), *many(2, line + (2, T, D), BF16),
            VM((4, t2, 768), BF16), VM((4, t2, 512), BF16), VM((4, 2, 192, t2), BF16), VM((4, 2, 128, t2), BF16),
            VM((3,) + cube + (64, 256), F32), VM((2,) + cube + (64, 256), F32), VM((2, 192, D), F32),
            VM((2, 128, D), F32), VM((3,) + square + (64, 256), F32), VM((2,) + square + (64, 256), F32),
            VM((192, D), F32), VM((128, D), F32), VM((16, 24, 128), F32),
            *[dma((spreads, 3))] * 2, *[dma((spreads, 4))] * 2, dma((spreads,)), *[dma((10,))] * 3, *[dma((20,))] * 2,
        ],
        compiler_params=pltpu.CompilerParams(collective_id=0, has_side_effects=True, vmem_limit_bytes=HIGH_VMEM),
    )(x, dy, trig, gq, gk, gains, *weights)


def rope_tables(positions):
    inv_freq = ROPE_THETA ** (-2.0 * jnp.arange(HD // 2, dtype=F32) / HD)
    angle = positions.reshape(-1, 1).astype(F32) * inv_freq
    cos_half, sin_half = jnp.cos(angle), jnp.sin(angle)
    return jnp.concatenate([cos_half, cos_half, -sin_half, sin_half], axis=-1)


def solution(mesh):
    axis_name = mesh.axis_names[0]
    sharded = P(axis_name)
    in_specs = (sharded,) * 5 + (P(), P()) + (sharded,) * 7
    out_specs = (sharded,) * 4 + (P(), P()) + (sharded,) * 7

    def device_step(hidden, grad_out, positions, norm1, norm2, gain_q, gain_k, w_q, w_k, w_v, w_o, w_gate, w_up, w_down):
        trig = rope_tables(positions)
        gains = jnp.broadcast_to(jnp.concatenate([norm1, norm2]).astype(F32)[None, :], (8, 128))
        x, dy = hidden.reshape(T, D), grad_out.reshape(T, D)
        gq, gk = gain_q.astype(F32)[None, :], gain_k.astype(F32)[None, :]
        out, d_hidden, d_qkv, d_gate_up, d_wo, d_wd, g_sum = layer_call(
            x, dy, trig, gq, gk, gains, w_q, w_k, w_v, w_o, w_gate, w_up, w_down
        )
        start = lax.axis_index(axis_name) * 64
        d_norm1 = lax.dynamic_slice(g_sum[:8].reshape(D), (start,), (64,))
        d_norm2 = lax.dynamic_slice(g_sum[8:16].reshape(D), (start,), (64,))
        return (
            out.reshape(hidden.shape), d_hidden.reshape(hidden.shape), d_norm1, d_norm2, g_sum[16], g_sum[17],
            d_qkv[:, :NQ], d_qkv[:, NQ : NQ + D], d_qkv[:, NQ + D :], d_wo, d_gate_up[:, :FF], d_gate_up[:, FF:], d_wd,
        )

    return jax.shard_map(device_step, mesh=mesh, in_specs=in_specs, out_specs=out_specs, check_vma=False)
```

time: 1170 us -> 227 us (0.19)
  waiting for transfers between devices: 885 us -> 0 us
  Pallas kernels: 0 us -> 210 us
  matrix products: 107 us -> 0 us
  blocking collectives: 99.2 us -> 0 us
  other arithmetic: 25.5 us -> 3.69 us
  local copies, waits for them, and re-layouts: 30.8 us -> 11.9 us
  between operations: 15.4 us -> 0.69 us
    reduce_scatter x7 -> x0, waiting for transfers between devices: 570 us -> none  [device_step(): lax.psum_scatter(row_grad * inv_tokens, axis_name, scatter_dimension=0, t...]
    all_gather x14 -> x0, waiting for transfers between devices: 307 us -> none  [gather_weights(): lax.all_gather(row_shard, axis_name, axis=0, tiled=True)]
    pallas_call x0 -> x1, Pallas kernels: none -> 210 us  [layer_call(): pl.pallas_call(layer_kernel, name='layer', out_shape=(shape(T, D, BF16),...]
    dot_general x26 -> x0, matrix products: 105 us -> none  [the longest x7 35.7 us: matmul_tn(): lax.dot_general(left_op, right_op, (((0,), (0,)), ((), ())), preferred_el...]
    unnamed x3 -> x0, blocking collectives: 99.2 us -> none
  transfers between devices with their start and end apart: 21 -> 0, of which waited for: 17 -> 0; matrix products, arithmetic and copies ran while one was open for 13% -> 0% of each run, Pallas kernels for 0% -> 0%
where the time goes in v2:
time: 227 us; the launch traced here: 226 us
  Pallas kernels  210 us (93%)
  local copies, waits for them, and re-layouts  11.9 us (5%)
  other arithmetic  3.69 us (2%)
    pallas_call x1, Pallas kernels, layer_call(): pl.pallas_call(layer_kernel, name='layer', out_shape=(shape(T, D, BF16),...  210 us

profile of v2, /device:TPU:0, one launch (start us, length us, event | category | flops | bytes accessed | tf_op | source)
XLA Modules:
  0.0 226.2 jit_solution(11063035670558301236)
XLA Ops:
  0.6 0.7 convert_bitcast_fusion
  1.3 0.7 maximum_convert_fusion
  2.1 1.2 bitcast_convert_fusion
  3.3 0.6 broadcast_in_dim.21.gains
  3.9 0.3 multiply_cosine_fusion
  4.2 0.8 pad_maximum_fusion.trig_ref
  4.9 210.0 %layer.1 = (bf16[128,1024]{1,0:T(8,128)(2,1)}, bf16[128,1024]{1,0:T(8,128)(2,1)}, f32[64,4096]{1,0:T(8,128)}, f32[64,6144]{1,0:T(8,128)}, f32[128,1024]{1,0:T(8,...) custom-call(bf16[128,1024]{1,0:T(8,128)(2,1)} %bitcast.20, bf16[128,1024]{1,0:T(8,128)(2,1)} %bitcast.21, ...), custom_call_target="tpu_custom_call" | custom-call | tf_op jit(solution)/shard_map/layer/pallas_call | solution.py:695
  214.9 0.0 copy-start
  214.9 1.3 slice_bitcast_fusion.2
  216.3 0.7 slice_bitcast_fusion
  217.0 0.6 dynamic_slice.7
  217.5 0.6 dynamic_slice.6
  218.1 1.9 slice.31
  220.0 1.9 fusion.2
  221.9 0.0 copy-done
  221.9 0.0 copy-start.4
  221.9 0.0 copy-start.3
  221.9 0.0 copy-start.2
  221.9 1.3 fusion.1
  223.1 0.0 copy-start.1
  223.1 0.0 copy-done.4
  223.1 0.7 copy.32
  223.8 0.0 copy-done.3
  223.8 0.7 copy.33
  224.5 0.0 copy-done.2
  224.6 0.8 copy.34
  225.3 0.0 copy-done.1
  225.3 0.9 copy.35
  (1 shorter events, 0.0 us)
Async XLA Ops:
  214.9 6.9 %copy-start = (f32[64,6144]{1,0:T(8,128)S(1)}, f32[64,6144]{1,0:T(8,128)}, u32[]{:S(2)}) copy-start(f32[64,6144]{1,0:T(8,128)} %get-tuple-element.25) | copy-start | bytes 4718596
  221.9 1.3 copy-start.4
  221.9 2.0 copy-start.3
  221.9 2.7 %copy-start.2 = (f32[128,1024]{1,0:T(8,128)S(1)}, f32[128,1024]{1,0:T(8,128)}, u32[]{:S(2)}) copy-start(f32[128,1024]{1,0:T(8,128)} %get-tuple-element.62) | copy-start | bytes 1572868
  223.1 2.2 copy-start.1

commit v3 on v2

--- a/solution.py
+++ b/solution.py
@@ -263,7 +263,6 @@
             made.append(spread(src.at[rows], None, buf, (rows, ALL), turns[i], (Y, X, C)))
         return made
 
-    gain_part = spread(gains, None, gbuf, both, (X, Y, Z), (Z, Y, X, C))
     p_qkv = by_columns(wq, bq) + by_columns(wk, bk) + by_columns(wv, bv)
     p_o, p_d = by_rows(wo, bo), by_rows(wd, bd)
     p_g, p_u = by_columns(wg, bg), by_columns(wu, bu)
@@ -284,7 +283,7 @@
     e_qkv = share(1, grp_y, cols_for(grp_y, dqkv, 512), qkvbuf)
     e_a = share(2, grp_y, lambda bit: at_ref.at[bit[Y], :, bit[C]], abuf)
     e_c = share(3, grp_x, lambda bit: ct_ref.at[:, bit[X], bit[C]], cbuf)
-    gain_number = 9
+    gain_number, norm_number = 9, 10
     sent = []
 
     def near_copy(dim, source, target):
@@ -309,13 +308,19 @@
 
     pl.semaphore_wait(barrier, 15)
 
-    def gain_copy(k):
-        return pltpu.make_async_remote_copy(
-            src_ref=gpart, dst_ref=gainbuf.at[me], send_sem=one_send.at[gain_number],
-            recv_sem=one_recv.at[gain_number], device_id=other(k), device_id_type=MESH,
-        )
-
-    gain_part.begin()
+    def to_all(source, buf, number):
+        @each(15)
+        def _(k):
+            pltpu.make_async_remote_copy(
+                src_ref=source, dst_ref=buf.at[me], send_sem=one_send.at[number], recv_sem=one_recv.at[number],
+                device_id=other(k + 1), device_id_type=MESH,
+            ).start()
+
+    def all_wait(buf, sem):
+        fifteen = buf.at[pl.ds(0, 15)]
+        pltpu.make_async_copy(fifteen, fifteen, sem).wait()
+
+    to_all(gains, gbuf, norm_number)
     for item in p_qkv + p_o:
         item.begin()
     x_copy = near_copy(Z, x_ref, xp.at[mine])
@@ -324,24 +329,21 @@
     trig_copy.start()
     xp[mine] = x_ref[...]
     trig[z] = trig_ref[...]
-    for step in range(3):
-        gain_part.advance(step)
-    for item in p_o + p_qkv:
-        item.advance(0)
-    for item in p_g + p_u:
+    for item in p_d + p_g + p_u:
         item.begin()
     dy_copy = near_copy(Z, dy_ref, dybuf.at[y, c, z])
     dy_copy.start()
     dybuf[y, c, z] = dy_ref[...]
-    gain_part.arrived()
+    for item in p_qkv + p_o:
+        item.advance(0)
+    all_wait(gbuf, one_recv.at[norm_number])
+    gbuf[me] = gains[...]
     lane = lax.broadcasted_iota(jnp.int32, (8, 128), 1) < 64
     for i in range(8):
-        first, second = gbuf[i // 4, (i // 2) % 2, i % 2, 0], gbuf[i // 4, (i // 2) % 2, i % 2, 1]
+        first, second = gbuf[2 * i], gbuf[2 * i + 1]
         tile = slice(128 * i, 128 * i + 128)
         g1[:, tile] = jnp.where(lane, first, pltpu.roll(second, 64, axis=1))[:1]
         g2[:, tile] = jnp.where(lane, pltpu.roll(first, 64, axis=1), second)[:1]
-    for item in p_qkv:
-        item.advance(1)
     x_copy.wait_recv()
 
     @each(8)
@@ -353,19 +355,21 @@
     def turned(val):
         return val.astype(F32).T.astype(BF16)
 
+    for item in p_qkv:
+        item.advance(1)
+    for item in p_d:
+        item.advance(0)
+
+    @each(4)
+    def _(i):
+        nbuf[y, c, cols(i, 256)] = turned(n_s[:, cols(i, 256)])
+
     for item in p_o:
         item.advance(1)
-    for item in p_d:
-        item.begin()
-
-    @each(4)
-    def _(i):
-        nbuf[y, c, cols(i, 256)] = turned(n_s[:, cols(i, 256)])
-
+    for item in p_g + p_u:
+        item.advance(0)
     for item in p_qkv:
         item.advance(2)
-    for item in p_d + p_g + p_u:
-        item.advance(0)
     trig_copy.wait_recv()
 
     def weight(buf, tile):
@@ -577,9 +581,6 @@
             out[half, :, tile] = nn(left, weight(right_buf, tile)) * inv_tokens
 
     p_m.advance(0)
-    p_n.advance(0)
-    p_dy.advance(0)
-    p_dr.advance(0)
     p_m.arrived()
     e_gu.arrived()
     gu_far = []
@@ -587,6 +588,7 @@
         column_chunk(mbuf, gubuf, rgu, chunk)
         gu_far.append(near_copy(Y, half_of(Y, rgu, chunk), zgu.at[chunk]))
         gu_far[-1].start()
+    p_n.advance(0)
     p_n.arrived()
     e_qkv.arrived()
     qkv_far = []
@@ -594,11 +596,13 @@
         column_chunk(nbuf, qkvbuf, rqkv, chunk)
         qkv_far.append(near_copy(X, half_of(X, rqkv, chunk), zqkv.at[chunk]))
         qkv_far[-1].start()
+    p_dy.advance(0)
     p_dy.arrived()
     e_a.arrived()
     row_tiles(abuf, dybuf, rwd)
     wd_far = near_copy(X, rwd.at[1 - x], zwd)
     wd_far.start()
+    p_dr.advance(0)
     p_dr.arrived()
     e_c.arrived()
     row_tiles(cbuf, drbuf, rwo)
@@ -625,10 +629,7 @@
     gpart[17:18, :] = k_total
     gpart[18:24, :] = jnp.zeros((6, 128), F32)
 
-    @each(15)
-    def _(k):
-        gain_copy(k + 1).start()
-
+    to_all(gpart, gainbuf, gain_number)
     received(y_copies)
 
     @each(4)
@@ -664,17 +665,22 @@
     owd[...] = rwd[x] + zwd[...]
     wo_far.wait_recv()
     owo[...] = rwo[y] + zwo[...]
-    fifteen = gainbuf.at[pl.ds(0, 15)]
-    pltpu.make_async_copy(fifteen, fifteen, one_recv.at[gain_number]).wait()
+    all_wait(gainbuf, one_recv.at[gain_number])
     gainbuf[me] = gpart[...]
-    ogain[...] = loop(16, lambda i, total: total + gainbuf[i], jnp.zeros((24, 128), F32)) * inv_tokens
+    gainbuf[0] = loop(16, lambda i, total: total + gainbuf[i], jnp.zeros((24, 128), F32)) * inv_tokens
+    for i in range(2):
+        row = gainbuf[0, pl.ds(8 * i + lax.div(me, 2), 1), :]
+        ogain[i : i + 1, :] = jnp.where(c == 0, row, pltpu.roll(row, 64, axis=1))
+    ogain[2:4, :] = gainbuf[0, 16:18, :]
+    ogain[4:8, :] = jnp.zeros((4, 128), F32)
     for move in moves:
         move.arrived()
     for item in moves + [e_gu, e_qkv, e_a, e_c] + parts:
         item.drain()
     for copy in sent:
         copy.wait_send()
-    pltpu.make_async_copy(fifteen, fifteen, one_send.at[gain_number]).wait()
+    all_wait(gainbuf, one_send.at[gain_number])
+    all_wait(gbuf, one_send.at[norm_number])
 
 
 def shape(rows, width, dtype):
@@ -691,18 +697,18 @@
     dma = pltpu.SemaphoreType.DMA
     t2, kvh, fh = 2 * T, D // 2, FF // 2
     cube, square, line = (2, 2, 2, 2), (2, 2, 2), (2, 2)
-    spreads = 19
+    spreads = 18
     return pl.pallas_call(
         layer_kernel,
         name="layer",
         out_shape=(
             shape(T, D, BF16), shape(T, D, BF16), shape(64, NQ + 2 * D, F32), shape(64, 2 * FF, F32),
-            shape(128, D, F32), shape(192, D, F32), shape(24, 128, F32),
+            shape(128, D, F32), shape(192, D, F32), shape(8, 128, F32),
         ),
-        in_specs=[vmem] * 5 + [hbm] * 8,
+        in_specs=[vmem] * 6 + [hbm] * 7,
         out_specs=(vmem, vmem, hbm, hbm, vmem, vmem, vmem),
         scratch_shapes=[
-            VM(cube + (8, 128), F32), VM(cube + (64, D), BF16), *many(2, cube + (64, kvh), BF16),
+            VM((16, 8, 128), F32), VM(cube + (64, D), BF16), *many(2, cube + (64, kvh), BF16),
             VM(square + (128, D), BF16), *many(2, cube + (64, fh), BF16), VM(square + (192, D), BF16),
             *many(2, (1, D), F32),
             VM((t2, D), BF16), VM((2, T, t2), F32), VM((t2, D), BF16), VM((t2, D), BF16), *many(2, (t2, kvh), BF16),
@@ -715,10 +721,45 @@
             VM((3,) + cube + (64, 256), F32), VM((2,) + cube + (64, 256), F32), VM((2, 192, D), F32),
             VM((2, 128, D), F32), VM((3,) + square + (64, 256), F32), VM((2,) + square + (64, 256), F32),
             VM((192, D), F32), VM((128, D), F32), VM((16, 24, 128), F32),
-            *[dma((spreads, 3))] * 2, *[dma((spreads, 4))] * 2, dma((spreads,)), *[dma((10,))] * 3, *[dma((20,))] * 2,
+            *[dma((spreads, 3))] * 2, *[dma((spreads, 4))] * 2, dma((spreads,)), *[dma((11,))] * 3, *[dma((20,))] * 2,
         ],
         compiler_params=pltpu.CompilerParams(collective_id=0, has_side_effects=True, vmem_limit_bytes=HIGH_VMEM),
     )(x, dy, trig, gq, gk, gains, *weights)
+
+
+def deliver_kernel(y_in, dh_in, qkv_in, gu_in, wo_in, wd_in, gain_in, *refs):
+    outs, gains_out, scratch, (in_sem, out_sem) = refs[:9], refs[9:13], refs[13:22], refs[22:]
+    spans = ((qkv_in, 0, NQ), (qkv_in, NQ, D), (qkv_in, NQ + D, D), (gu_in, 0, FF), (gu_in, FF, FF))
+    q_in, k_in, v_in, g_in, u_in = (ref.at[:, pl.ds(start, size)] for ref, start, size in spans)
+    sources = (y_in, dh_in, q_in, k_in, v_in, wo_in, g_in, u_in, wd_in)
+    loads = [pltpu.make_async_copy(src, buf, in_sem.at[i]) for i, (src, buf) in enumerate(zip(sources, scratch))]
+    stores = [pltpu.make_async_copy(buf, out, out_sem.at[i]) for i, (buf, out) in enumerate(zip(scratch, outs))]
+    for load in loads:
+        load.start()
+    for i, out in enumerate(gains_out):
+        out[...] = gain_in[i : i + 1, : out.shape[0]].reshape(out.shape)
+    for load, store in zip(loads, stores):
+        load.wait()
+        store.start()
+    for store in stores:
+        store.wait()
+
+
+def deliver(*results):
+    vmem = pl.BlockSpec(memory_space=VM)
+    hbm = pl.BlockSpec(memory_space=pl.ANY)
+    dma = pltpu.SemaphoreType.DMA
+    sizes = [(T, D, BF16)] * 2 + [(64, width, F32) for width in (NQ, D, D)] + [(128, D, F32)]
+    sizes += [(64, FF, F32)] * 2 + [(192, D, F32)]
+    small = [jax.ShapeDtypeStruct((size,), F32) for size in (64, 64, 128, 128)]
+    return pl.pallas_call(
+        deliver_kernel,
+        name="deliver",
+        out_shape=tuple([shape(*size) for size in sizes] + small),
+        in_specs=[hbm] * 6 + [vmem],
+        out_specs=tuple([hbm] * 9 + [vmem] * 4),
+        scratch_shapes=[VM(size[:2], size[2]) for size in sizes] + [dma((9,)), dma((9,))],
+    )(*results)
 
 
 def rope_tables(positions):
@@ -739,15 +780,9 @@
         gains = jnp.broadcast_to(jnp.concatenate([norm1, norm2]).astype(F32)[None, :], (8, 128))
         x, dy = hidden.reshape(T, D), grad_out.reshape(T, D)
         gq, gk = gain_q.astype(F32)[None, :], gain_k.astype(F32)[None, :]
-        out, d_hidden, d_qkv, d_gate_up, d_wo, d_wd, g_sum = layer_call(
-            x, dy, trig, gq, gk, gains, w_q, w_k, w_v, w_o, w_gate, w_up, w_down
-        )
-        start = lax.axis_index(axis_name) * 64
-        d_norm1 = lax.dynamic_slice(g_sum[:8].reshape(D), (start,), (64,))
-        d_norm2 = lax.dynamic_slice(g_sum[8:16].reshape(D), (start,), (64,))
-        return (
-            out.reshape(hidden.shape), d_hidden.reshape(hidden.shape), d_norm1, d_norm2, g_sum[16], g_sum[17],
-            d_qkv[:, :NQ], d_qkv[:, NQ : NQ + D], d_qkv[:, NQ + D :], d_wo, d_gate_up[:, :FF], d_gate_up[:, FF:], d_wd,
-        )
+        results = layer_call(x, dy, trig, gq, gk, gains, w_q, w_k, w_v, w_o, w_gate, w_up, w_down)
+        out, d_hidden, d_wq, d_wk, d_wv, d_wo, d_wg, d_wu, d_wd, d_n1, d_n2, d_qn, d_kn = deliver(*results)
+        out, d_hidden = out.reshape(hidden.shape), d_hidden.reshape(hidden.shape)
+        return out, d_hidden, d_n1, d_n2, d_qn, d_kn, d_wq, d_wk, d_wv, d_wo, d_wg, d_wu, d_wd
 
     return jax.shard_map(device_step, mesh=mesh, in_specs=in_specs, out_specs=out_specs, check_vma=False)

time: 227 us -> 202 us (0.89)
  Pallas kernels: 210 us -> 197 us
  local copies, waits for them, and re-layouts: 11.9 us -> 0.59 us
    pallas_call x1, Pallas kernels: 210 us -> 192 us  [layer_call(): pl.pallas_call(layer_kernel, name='layer', out_shape=(shape(T, D, BF16),...]
    pallas_call x0 -> x1, Pallas kernels: none -> 5.41 us  [deliver(): pl.pallas_call(deliver_kernel, name='deliver', out_shape=tuple([shape(*si...]
    slice x3 -> x0, local copies, waits for them, and re-layouts: 4.99 us -> none  [the longest x1 1.87 us: device_step(): d_qkv[:, :NQ]]
    unnamed x14 -> x0, local copies, waits for them, and re-layouts: 3.1 us -> none
where the time goes in v3:
time: 202 us
  Pallas kernels  197 us (98%)
  other arithmetic  3.69 us (2%)
    pallas_call x1, Pallas kernels, layer_call(): pl.pallas_call(layer_kernel, name='layer', out_shape=(shape(T, D, BF16),...  192 us
    pallas_call x1, Pallas kernels, deliver(): pl.pallas_call(deliver_kernel, name='deliver', out_shape=tuple([shape(*si...  5.41 us

profile of v3, /device:TPU:0, one launch (start us, length us, event | category | flops | bytes accessed | tf_op | source)
XLA Modules:
  0.0 201.9 jit_solution(14391555729519540836)
XLA Ops:
  0.6 0.7 convert_bitcast_fusion
  1.3 0.7 maximum_convert_fusion
  2.1 1.2 bitcast_convert_fusion
  3.3 0.6 broadcast_in_dim.21.gains
  3.8 0.3 multiply_cosine_fusion
  4.2 0.8 pad_maximum_fusion.trig_ref
  4.9 191.6 %layer.1 = (bf16[128,1024]{1,0:T(8,128)(2,1)}, bf16[128,1024]{1,0:T(8,128)(2,1)}, f32[64,4096]{1,0:T(8,128)}, f32[64,6144]{1,0:T(8,128)}, f32[128,1024]{1,0:T(8,...) custom-call(bf16[128,1024]{1,0:T(8,128)(2,1)} %bitcast.12, bf16[128,1024]{1,0:T(8,128)(2,1)} %bitcast.13, ...), custom_call_target="tpu_custom_call" | custom-call | tf_op jit(solution)/shard_map/layer/pallas_call | solution.py:701
  196.5 5.4 %deliver.1 = (bf16[128,1024]{1,0:T(8,128)(2,1)}, bf16[128,1024]{1,0:T(8,128)(2,1)}, f32[64,2048]{1,0:T(8,128)}, f32[64,1024]{1,0:T(8,128)}, f32[64,1024]{1,0:T(8...) custom-call(bf16[128,1024]{1,0:T(8,128)(2,1)} %get-tuple-element.33., ...), custom_call_target="tpu_custom_call" | custom-call | tf_op jit(solution)/shard_map/deliver/pallas_call | solution.py:755
  (1 shorter events, 0.0 us)

commit v4 on v3

--- a/solution.py
+++ b/solution.py
@@ -222,9 +222,9 @@
 
 
 def layer_kernel(
-    x_ref, dy_ref, trig_ref, gq_ref, gk_ref, gains, wq, wk, wv, wo, wg, wu, wd,
+    cos_ref, sin_ref, n1_ref, n2_ref, qn_ref, kn_ref, x_ref, dy_ref, wq, wk, wv, wo, wg, wu, wd,
     y_ref, dh_ref, oqkv, ogu, owo, owd, ogain,
-    gbuf, bq, bk, bv, bo, bg, bu, bd, g1, g2,
+    gains, gbuf, bq, bk, bv, bo, bg, bu, bd, g1, g2,
     xp, trig, n_s, q_s, k_s, v_s, qr, kr, probs, ctx, h_s, m_s, spare, act, dact, dctx, dres,
     part_a, part_y, part_m, part_n, land_a, land_y, land_m, land_n,
     at_ref, ct_ref, dqkv, dgu, gpart,
@@ -296,7 +296,11 @@
         )
         return sent[-1]
 
-    mine, theirs = cols(z, T), cols(1 - z, T)
+    mine = cols(z, T)
+
+    def pair_rows(i):
+        return cols(4 * z + i, 32)
+
     barrier = pltpu.get_barrier_semaphore()
 
     def other(k):
@@ -306,6 +310,13 @@
     def _(k):
         pl.semaphore_signal(barrier, inc=1, device_id=other(k + 1), device_id_type=MESH)
 
+    gains[...] = jnp.zeros((8, 128), F32)
+    halves = [ref[...].astype(F32).reshape(1, 64) for ref in (n1_ref, n2_ref)]
+    gains[0:1, :] = jnp.concatenate(halves, axis=1)
+    gains[1:2, :] = qn_ref[...].astype(F32).reshape(1, 128)
+    gains[2:3, :] = kn_ref[...].astype(F32).reshape(1, 128)
+    cos_half, sin_half = cos_ref[...], sin_ref[...]
+    trig[z] = jnp.concatenate([cos_half, cos_half, -sin_half, sin_half], axis=1)
     pl.semaphore_wait(barrier, 15)
 
     def to_all(source, buf, number):
@@ -324,18 +335,20 @@
     for item in p_qkv + p_o:
         item.begin()
     x_copy = near_copy(Z, x_ref, xp.at[mine])
-    trig_copy = near_copy(Z, trig_ref, trig.at[z])
+    trig_copy = near_copy(Z, trig.at[z], trig.at[z])
     x_copy.start()
-    trig_copy.start()
-    xp[mine] = x_ref[...]
-    trig[z] = trig_ref[...]
+    own_x = pltpu.make_async_copy(x_ref, xp.at[mine], local_sem.at[len(parts)])
+    own_x.start()
     for item in p_d + p_g + p_u:
         item.begin()
+    trig_copy.start()
     dy_copy = near_copy(Z, dy_ref, dybuf.at[y, c, z])
     dy_copy.start()
-    dybuf[y, c, z] = dy_ref[...]
+    own_dy = pltpu.make_async_copy(dy_ref, dybuf.at[y, c, z], local_sem.at[len(parts) + 1])
+    own_dy.start()
     for item in p_qkv + p_o:
         item.advance(0)
+    gq, gk = gains[1:2, :], gains[2:3, :]
     all_wait(gbuf, one_recv.at[norm_number])
     gbuf[me] = gains[...]
     lane = lax.broadcasted_iota(jnp.int32, (8, 128), 1) < 64
@@ -344,6 +357,7 @@
         tile = slice(128 * i, 128 * i + 128)
         g1[:, tile] = jnp.where(lane, first, pltpu.roll(second, 64, axis=1))[:1]
         g2[:, tile] = jnp.where(lane, pltpu.roll(first, 64, axis=1), second)[:1]
+    own_x.wait()
     x_copy.wait_recv()
 
     @each(8)
@@ -397,11 +411,11 @@
     def _(j):
         seq, _, rows, kv, pair = sequence_head(j)
         cos, sin = trig[seq, :, :HD], trig[seq, :, HD:]
-        k_rot = head_forward(k_s[rows, kv], gk_ref[...], cos, sin)
+        k_rot = head_forward(k_s[rows, kv], gk, cos, sin)
         kr[rows, kv] = k_rot
         q_pair = q_s[rows, pair]
         q_rot = jnp.concatenate(
-            [head_forward(half, gq_ref[...], cos, sin) for half in (q_pair[:, :HD], q_pair[:, HD:])], axis=0
+            [head_forward(half, gq, cos, sin) for half in (q_pair[:, :HD], q_pair[:, HD:])], axis=0
         )
         qr[j] = q_rot
         scores = nt(q_rot, k_rot) * scale
@@ -449,23 +463,33 @@
     def _(i):
         rows = cols(i, 32)
         attn = (part_a[z, rows] + land_a[rows]).astype(BF16)
-        val = (x_ref[rows].astype(F32) + attn.astype(F32)).astype(BF16).astype(F32)
+        val = (xp[pair_rows(i)].astype(F32) + attn.astype(F32)).astype(BF16).astype(F32)
         h_s[rows] = val
-        m_s[pl.ds(pl.multiple_of(z * T + i * 32, 32), 32)] = (val * rms(val) * g2[...]).astype(BF16)
+        m_s[pair_rows(i)] = (val * rms(val) * g2[...]).astype(BF16)
 
     m_copy = near_copy(Z, m_s.at[mine], m_s.at[mine])
     m_copy.start()
     for item in p_d:
         item.arrived()
+    own_dy.wait()
     dy_copy.wait_recv()
 
     @each(4)
     def _(i):
         dact[:, cols(i, 384)] = nt(dybuf[y, c].reshape(2 * T, D), bd[two(i)].reshape(384, D))
 
+    m_copy.wait_recv()
+
+    @each(4)
+    def _(i):
+        mbuf[x, c, cols(i, 256)] = turned(m_s[:, cols(i, 256)])
+
     for item in p_g + p_u:
         item.advance(2)
-    m_copy.wait_recv()
+    p_m.begin()
+    p_n.begin()
+    p_dy.begin()
+    e_c.begin()
     for item in p_g + p_u:
         item.arrived()
     fh = FF // 2
@@ -485,23 +509,14 @@
         rows = two(i)
         return nt(dgu[:, :fh], bg[rows].reshape(256, fh)) + nt(dgu[:, fh:], bu[rows].reshape(256, fh))
 
+    e_gu.begin()
     m_copies = pair_sum(part_m, land_m, d_mlp_in)
-    e_gu.begin()
-
-    @each(4)
-    def _(i):
-        mbuf[x, c, cols(i, 256)] = turned(m_s[:, cols(i, 256)])
-
-    p_m.begin()
-    p_n.begin()
-    p_dy.begin()
 
     @each(4)
     def _(i):
         at_ref[two(i)] = turned(act[:, cols(i, 384)]).reshape(2, 192, 2 * T)
 
     e_a.begin()
-    e_c.begin()
     received(m_copies)
 
     def d_res_rows(i, total):
@@ -510,7 +525,7 @@
         r_scale = rms(val)
         unit = val * r_scale
         grad = part_m[z, rows] + land_m[rows]
-        out = dy_ref[rows].astype(F32) + norm_backward(grad * g2[...], unit, r_scale)
+        out = dybuf[y, c, z, rows].astype(F32) + norm_backward(grad * g2[...], unit, r_scale)
         dres[rows] = out
         drbuf[x, c, z, rows] = out.astype(BF16)
         return total + jnp.sum(grad * unit, axis=0, keepdims=True)
@@ -540,9 +555,9 @@
         d_q_rot = nn(d_score, kr[rows, kv])
         d_k_rot = tn(d_score, qr[j])
         q_pair = q_s[rows, pair]
-        d_q0, g_q0 = head_backward(d_q_rot[:T], q_pair[:, :HD], gq_ref[...], cos, sin)
-        d_q1, g_q1 = head_backward(d_q_rot[T:], q_pair[:, HD:], gq_ref[...], cos, sin)
-        d_k, g_k = head_backward(d_k_rot, k_s[rows, kv], gk_ref[...], cos, sin)
+        d_q0, g_q0 = head_backward(d_q_rot[:T], q_pair[:, :HD], gq, cos, sin)
+        d_q1, g_q1 = head_backward(d_q_rot[T:], q_pair[:, HD:], gq, cos, sin)
+        d_k, g_k = head_backward(d_k_rot, k_s[rows, kv], gk, cos, sin)
         dqkv[rows, pair] = jnp.concatenate([d_q0, d_q1], axis=1)
         dqkv[rows, cols(head + 8, HD)] = d_k
         dqkv[rows, cols(head + 12, HD)] = d_value
@@ -613,7 +628,7 @@
 
     def d_hidden_rows(i, total):
         rows = cols(i, 32)
-        val = x_ref[rows].astype(F32)
+        val = xp[pair_rows(i)].astype(F32)
         x_scale = rms(val)
         unit = val * x_scale
         grad = part_n[z, rows] + land_n[rows]
@@ -691,7 +706,7 @@
     return [VM(*args)] * count
 
 
-def layer_call(x, dy, trig, gq, gk, gains, *weights):
+def layer_call(*operands):
     vmem = pl.BlockSpec(memory_space=VM)
     hbm = pl.BlockSpec(memory_space=pl.ANY)
     dma = pltpu.SemaphoreType.DMA
@@ -705,10 +720,10 @@
             shape(T, D, BF16), shape(T, D, BF16), shape(64, NQ + 2 * D, F32), shape(64, 2 * FF, F32),
             shape(128, D, F32), shape(192, D, F32), shape(8, 128, F32),
         ),
-        in_specs=[vmem] * 6 + [hbm] * 7,
+        in_specs=[vmem] * 6 + [hbm] * 9,
         out_specs=(vmem, vmem, hbm, hbm, vmem, vmem, vmem),
         scratch_shapes=[
-            VM((16, 8, 128), F32), VM(cube + (64, D), BF16), *many(2, cube + (64, kvh), BF16),
+            VM((8, 128), F32), VM((16, 8, 128), F32), VM(cube + (64, D), BF16), *many(2, cube + (64, kvh), BF16),
             VM(square + (128, D), BF16), *many(2, cube + (64, fh), BF16), VM(square + (192, D), BF16),
             *many(2, (1, D), F32),
             VM((t2, D), BF16), VM((2, T, t2), F32), VM((t2, D), BF16), VM((t2, D), BF16), *many(2, (t2, kvh), BF16),
@@ -721,10 +736,10 @@
             VM((3,) + cube + (64, 256), F32), VM((2,) + cube + (64, 256), F32), VM((2, 192, D), F32),
             VM((2, 128, D), F32), VM((3,) + square + (64, 256), F32), VM((2,) + square + (64, 256), F32),
             VM((192, D), F32), VM((128, D), F32), VM((16, 24, 128), F32),
-            *[dma((spreads, 3))] * 2, *[dma((spreads, 4))] * 2, dma((spreads,)), *[dma((11,))] * 3, *[dma((20,))] * 2,
+            *[dma((spreads, 3))] * 2, *[dma((spreads, 4))] * 2, dma((spreads + 2,)), *[dma((11,))] * 3, *[dma((20,))] * 2,
         ],
         compiler_params=pltpu.CompilerParams(collective_id=0, has_side_effects=True, vmem_limit_bytes=HIGH_VMEM),
-    )(x, dy, trig, gq, gk, gains, *weights)
+    )(*operands)
 
 
 def deliver_kernel(y_in, dh_in, qkv_in, gu_in, wo_in, wd_in, gain_in, *refs):
@@ -766,7 +781,7 @@
     inv_freq = ROPE_THETA ** (-2.0 * jnp.arange(HD // 2, dtype=F32) / HD)
     angle = positions.reshape(-1, 1).astype(F32) * inv_freq
     cos_half, sin_half = jnp.cos(angle), jnp.sin(angle)
-    return jnp.concatenate([cos_half, cos_half, -sin_half, sin_half], axis=-1)
+    return cos_half, sin_half
 
 
 def solution(mesh):
@@ -776,11 +791,9 @@
     out_specs = (sharded,) * 4 + (P(), P()) + (sharded,) * 7
 
     def device_step(hidden, grad_out, positions, norm1, norm2, gain_q, gain_k, w_q, w_k, w_v, w_o, w_gate, w_up, w_down):
-        trig = rope_tables(positions)
-        gains = jnp.broadcast_to(jnp.concatenate([norm1, norm2]).astype(F32)[None, :], (8, 128))
+        cos, sin = rope_tables(positions)
         x, dy = hidden.reshape(T, D), grad_out.reshape(T, D)
-        gq, gk = gain_q.astype(F32)[None, :], gain_k.astype(F32)[None, :]
-        results = layer_call(x, dy, trig, gq, gk, gains, w_q, w_k, w_v, w_o, w_gate, w_up, w_down)
+        results = layer_call(cos, sin, norm1, norm2, gain_q, gain_k, x, dy, w_q, w_k, w_v, w_o, w_gate, w_up, w_down)
         out, d_hidden, d_wq, d_wk, d_wv, d_wo, d_wg, d_wu, d_wd, d_n1, d_n2, d_qn, d_kn = deliver(*results)
         out, d_hidden = out.reshape(hidden.shape), d_hidden.reshape(hidden.shape)
         return out, d_hidden, d_n1, d_n2, d_qn, d_kn, d_wq, d_wk, d_wv, d_wo, d_wg, d_wu, d_wd

time: 202 us -> 193 us (0.955)
  Pallas kernels: 197 us -> 190 us
  other arithmetic: 3.69 us -> 1.64 us
    pallas_call x1, Pallas kernels: 192 us -> 185 us  [layer_call(): pl.pallas_call(layer_kernel, name='layer', out_shape=(shape(T, D, BF16),...]
where the time goes in v4:
time: 193 us
  Pallas kernels  190 us (98%)
    pallas_call x1, Pallas kernels, layer_call(): pl.pallas_call(layer_kernel, name='layer', out_shape=(shape(T, D, BF16),...  185 us
    pallas_call x1, Pallas kernels, deliver(): pl.pallas_call(deliver_kernel, name='deliver', out_shape=tuple([shape(*si...  5.41 us

profile of v4, /device:TPU:0, one launch (start us, length us, event | category | flops | bytes accessed | tf_op | source)
XLA Modules:
  0.0 192.8 jit_solution(8325940815086416192)
XLA Ops:
  0.6 0.7 convert_bitcast_fusion
  1.3 1.0 multiply_sine_fusion
  2.3 185.1 %layer.1 = (bf16[128,1024]{1,0:T(8,128)(2,1)}, bf16[128,1024]{1,0:T(8,128)(2,1)}, f32[64,4096]{1,0:T(8,128)}, f32[64,6144]{1,0:T(8,128)}, f32[128,1024]{1,0:T(8,...) custom-call(f32[128,64]{1,0:T(8,128)} %get-tuple-element.54.cos_ref, f32[128,64]{1,0:T(8,128)} %get-tuple-element.53.sin_ref, ...), custom_call_target="tpu_custom_call" | custom-call | tf_op jit(solution)/shard_map/layer/pallas_call | solution.py:716
  187.4 5.4 %deliver.1 = (bf16[128,1024]{1,0:T(8,128)(2,1)}, bf16[128,1024]{1,0:T(8,128)(2,1)}, f32[64,2048]{1,0:T(8,128)}, f32[64,1024]{1,0:T(8,128)}, f32[64,1024]{1,0:T(8...) custom-call(bf16[128,1024]{1,0:T(8,128)(2,1)} %get-tuple-element.33., ...), custom_call_target="tpu_custom_call" | custom-call | tf_op jit(solution)/shard_map/deliver/pallas_call | solution.py:770
  (1 shorter events, 0.0 us)

commit v5 on v4

--- a/solution.py
+++ b/solution.py
@@ -487,7 +487,6 @@
     for item in p_g + p_u:
         item.advance(2)
     p_m.begin()
-    p_n.begin()
     p_dy.begin()
     e_c.begin()
     for item in p_g + p_u:
@@ -517,6 +516,7 @@
         at_ref[two(i)] = turned(act[:, cols(i, 384)]).reshape(2, 192, 2 * T)
 
     e_a.begin()
+    p_n.begin()
     received(m_copies)
 
     def d_res_rows(i, total):
@@ -534,8 +534,24 @@
     r_copy = near_copy(Z, drbuf.at[x, c, z], drbuf.at[x, c, z])
     r_copy.start()
     y_copies = pair_sum(part_y, land_y, lambda i: nn(act[...], weight(bd, cols(i, 256))))
+    inv_tokens = 1.0 / (16 * T)
+
+    def row_tiles(left_buf, right_buf, out):
+        @each(8)
+        def _(j):
+            tile = cols(lax.rem(j, 4), 256)
+            half = lax.div(j, 4)
+            left = jnp.concatenate([left_buf[i, half] for i in range(4)], axis=1)
+            out[half, :, tile] = nn(left, weight(right_buf, tile)) * inv_tokens
+
+    p_dy.advance(0)
+    p_dy.arrived()
+    e_a.arrived()
+    row_tiles(abuf, dybuf, rwd)
     r_copy.wait_recv()
     p_dr.begin()
+    wd_far = near_copy(X, rwd.at[1 - x], zwd)
+    wd_far.start()
 
     @each(2)
     def _(i):
@@ -573,7 +589,6 @@
         return grad + nt(dqkv[:, D + 512 :], bv[rows].reshape(256, 512))
 
     n_copies = pair_sum(part_n, land_n, d_normed)
-    inv_tokens = 1.0 / (16 * T)
 
     def column_chunk(acts, grads, out, chunk):
         @each(8)
@@ -586,14 +601,6 @@
     def half_of(dim, result, chunk):
         bit = place.bit[dim]
         return result.at[(chunk,) + tuple(1 - bit if k == dim else ALL for k in range(4))]
-
-    def row_tiles(left_buf, right_buf, out):
-        @each(8)
-        def _(j):
-            tile = cols(lax.rem(j, 4), 256)
-            half = lax.div(j, 4)
-            left = jnp.concatenate([left_buf[i, half] for i in range(4)], axis=1)
-            out[half, :, tile] = nn(left, weight(right_buf, tile)) * inv_tokens
 
     p_m.advance(0)
     p_m.arrived()
@@ -611,12 +618,6 @@
         column_chunk(nbuf, qkvbuf, rqkv, chunk)
         qkv_far.append(near_copy(X, half_of(X, rqkv, chunk), zqkv.at[chunk]))
         qkv_far[-1].start()
-    p_dy.advance(0)
-    p_dy.arrived()
-    e_a.arrived()
-    row_tiles(abuf, dybuf, rwd)
-    wd_far = near_copy(X, rwd.at[1 - x], zwd)
-    wd_far.start()
     p_dr.advance(0)
     p_dr.arrived()
     e_c.arrived()

time: 193 us -> 191 us (0.990)
  Pallas kernels: 190 us -> 188 us
    pallas_call x1, Pallas kernels: 185 us -> 183 us  [layer_call(): pl.pallas_call(layer_kernel, name='layer', out_shape=(shape(T, D, BF16),...]
where the time goes in v5:
time: 191 us
  Pallas kernels  188 us (98%)
    pallas_call x1, Pallas kernels, layer_call(): pl.pallas_call(layer_kernel, name='layer', out_shape=(shape(T, D, BF16),...  183 us
    pallas_call x1, Pallas kernels, deliver(): pl.pallas_call(deliver_kernel, name='deliver', out_shape=tuple([shape(*si...  5.41 us

profile of v5, /device:TPU:0, one launch (start us, length us, event | category | flops | bytes accessed | tf_op | source)
XLA Modules:
  0.0 190.7 jit_solution(4205554913051655142)
XLA Ops:
  0.6 0.7 convert_bitcast_fusion
  1.3 1.0 multiply_sine_fusion
  2.3 183.0 %layer.1 = (bf16[128,1024]{1,0:T(8,128)(2,1)}, bf16[128,1024]{1,0:T(8,128)(2,1)}, f32[64,4096]{1,0:T(8,128)}, f32[64,6144]{1,0:T(8,128)}, f32[128,1024]{1,0:T(8,...) custom-call(f32[128,64]{1,0:T(8,128)} %get-tuple-element.54.cos_ref, f32[128,64]{1,0:T(8,128)} %get-tuple-element.53.sin_ref, ...), custom_call_target="tpu_custom_call" | custom-call | tf_op jit(solution)/shard_map/layer/pallas_call | solution.py:717
  185.3 5.4 %deliver.1 = (bf16[128,1024]{1,0:T(8,128)(2,1)}, bf16[128,1024]{1,0:T(8,128)(2,1)}, f32[64,2048]{1,0:T(8,128)}, f32[64,1024]{1,0:T(8,128)}, f32[64,1024]{1,0:T(8...) custom-call(bf16[128,1024]{1,0:T(8,128)(2,1)} %get-tuple-element.33., ...), custom_call_target="tpu_custom_call" | custom-call | tf_op jit(solution)/shard_map/deliver/pallas_call | solution.py:771
  (1 shorter events, 0.0 us)

commit v6 on v5

--- a/solution.py
+++ b/solution.py
@@ -222,7 +222,7 @@
 
 
 def layer_kernel(
-    cos_ref, sin_ref, n1_ref, n2_ref, qn_ref, kn_ref, x_ref, dy_ref, wq, wk, wv, wo, wg, wu, wd,
+    pos_ref, freq_ref, n1_ref, n2_ref, qn_ref, kn_ref, x_ref, dy_ref, wq, wk, wv, wo, wg, wu, wd,
     y_ref, dh_ref, oqkv, ogu, owo, owd, ogain,
     gains, gbuf, bq, bk, bv, bo, bg, bu, bd, g1, g2,
     xp, trig, n_s, q_s, k_s, v_s, qr, kr, probs, ctx, h_s, m_s, spare, act, dact, dctx, dres,
@@ -315,7 +315,8 @@
     gains[0:1, :] = jnp.concatenate(halves, axis=1)
     gains[1:2, :] = qn_ref[...].astype(F32).reshape(1, 128)
     gains[2:3, :] = kn_ref[...].astype(F32).reshape(1, 128)
-    cos_half, sin_half = cos_ref[...], sin_ref[...]
+    angle = jnp.broadcast_to(pos_ref[...].astype(F32), (T, T)).T[:, : HD // 2] * freq_ref[...]
+    cos_half, sin_half = jnp.cos(angle), jnp.sin(angle)
     trig[z] = jnp.concatenate([cos_half, cos_half, -sin_half, sin_half], axis=1)
     pl.semaphore_wait(barrier, 15)
 
@@ -744,17 +745,23 @@
 
 
 def deliver_kernel(y_in, dh_in, qkv_in, gu_in, wo_in, wd_in, gain_in, *refs):
-    outs, gains_out, scratch, (in_sem, out_sem) = refs[:9], refs[9:13], refs[13:22], refs[22:]
+    rest = iter(refs)
+    outs, small_outs, scratch, small = ([next(rest) for _ in range(count)] for count in (9, 4, 9, 4))
+    gain, in_sem, out_sem = rest
     spans = ((qkv_in, 0, NQ), (qkv_in, NQ, D), (qkv_in, NQ + D, D), (gu_in, 0, FF), (gu_in, FF, FF))
     q_in, k_in, v_in, g_in, u_in = (ref.at[:, pl.ds(start, size)] for ref, start, size in spans)
-    sources = (y_in, dh_in, q_in, k_in, v_in, wo_in, g_in, u_in, wd_in)
-    loads = [pltpu.make_async_copy(src, buf, in_sem.at[i]) for i, (src, buf) in enumerate(zip(sources, scratch))]
-    stores = [pltpu.make_async_copy(buf, out, out_sem.at[i]) for i, (buf, out) in enumerate(zip(scratch, outs))]
+    sources = (gain_in, y_in, dh_in, q_in, k_in, v_in, wo_in, g_in, u_in, wd_in)
+    buffers = [gain] + scratch
+    loads = [pltpu.make_async_copy(src, buf, in_sem.at[i]) for i, (src, buf) in enumerate(zip(sources, buffers))]
+    pairs = zip(small + scratch, small_outs + outs)
+    stores = [pltpu.make_async_copy(buf, out, out_sem.at[i]) for i, (buf, out) in enumerate(pairs)]
     for load in loads:
         load.start()
-    for i, out in enumerate(gains_out):
-        out[...] = gain_in[i : i + 1, : out.shape[0]].reshape(out.shape)
-    for load, store in zip(loads, stores):
+    loads[0].wait()
+    for i, (buf, store) in enumerate(zip(small, stores)):
+        buf[...] = gain[i : i + 1, : buf.shape[0]].reshape(buf.shape)
+        store.start()
+    for load, store in zip(loads[1:], stores[len(small) :]):
         load.wait()
         store.start()
     for store in stores:
@@ -762,27 +769,20 @@
 
 
 def deliver(*results):
-    vmem = pl.BlockSpec(memory_space=VM)
     hbm = pl.BlockSpec(memory_space=pl.ANY)
     dma = pltpu.SemaphoreType.DMA
     sizes = [(T, D, BF16)] * 2 + [(64, width, F32) for width in (NQ, D, D)] + [(128, D, F32)]
     sizes += [(64, FF, F32)] * 2 + [(192, D, F32)]
-    small = [jax.ShapeDtypeStruct((size,), F32) for size in (64, 64, 128, 128)]
+    small = (64, 64, 128, 128)
+    scratch = [VM(size[:2], size[2]) for size in sizes] + [VM((size,), F32) for size in small]
     return pl.pallas_call(
         deliver_kernel,
         name="deliver",
-        out_shape=tuple([shape(*size) for size in sizes] + small),
-        in_specs=[hbm] * 6 + [vmem],
-        out_specs=tuple([hbm] * 9 + [vmem] * 4),
-        scratch_shapes=[VM(size[:2], size[2]) for size in sizes] + [dma((9,)), dma((9,))],
+        out_shape=tuple([shape(*size) for size in sizes] + [jax.ShapeDtypeStruct((size,), F32) for size in small]),
+        in_specs=[hbm] * len(results),
+        out_specs=(hbm,) * len(scratch),
+        scratch_shapes=scratch + [VM((8, 128), F32), dma((16,)), dma((16,))],
     )(*results)
-
-
-def rope_tables(positions):
-    inv_freq = ROPE_THETA ** (-2.0 * jnp.arange(HD // 2, dtype=F32) / HD)
-    angle = positions.reshape(-1, 1).astype(F32) * inv_freq
-    cos_half, sin_half = jnp.cos(angle), jnp.sin(angle)
-    return cos_half, sin_half
 
 
 def solution(mesh):
@@ -792,9 +792,9 @@
     out_specs = (sharded,) * 4 + (P(), P()) + (sharded,) * 7
 
     def device_step(hidden, grad_out, positions, norm1, norm2, gain_q, gain_k, w_q, w_k, w_v, w_o, w_gate, w_up, w_down):
-        cos, sin = rope_tables(positions)
+        inv_freq = ROPE_THETA ** (-2.0 * jnp.arange(HD // 2, dtype=F32) / HD)
         x, dy = hidden.reshape(T, D), grad_out.reshape(T, D)
-        results = layer_call(cos, sin, norm1, norm2, gain_q, gain_k, x, dy, w_q, w_k, w_v, w_o, w_gate, w_up, w_down)
+        results = layer_call(positions, inv_freq[None, :], norm1, norm2, gain_q, gain_k, x, dy, w_q, w_k, w_v, w_o, w_gate, w_up, w_down)
         out, d_hidden, d_wq, d_wk, d_wv, d_wo, d_wg, d_wu, d_wd, d_n1, d_n2, d_qn, d_kn = deliver(*results)
         out, d_hidden = out.reshape(hidden.shape), d_hidden.reshape(hidden.shape)
         return out, d_hidden, d_n1, d_n2, d_qn, d_kn, d_wq, d_wk, d_wv, d_wo, d_wg, d_wu, d_wd

time: 191 us -> 189 us (0.990)
  no operation moved by 1% of the time
where the time goes in v6:
time: 189 us; the launch traced here: 188 us
  Pallas kernels  187 us (99%)
    pallas_call x1, Pallas kernels, layer_call(): pl.pallas_call(layer_kernel, name='layer', out_shape=(shape(T, D, BF16),...  183 us
    pallas_call x1, Pallas kernels, deliver(): pl.pallas_call(deliver_kernel, name='deliver', out_shape=tuple([shape(*si...  4.37 us

profile of v6, /device:TPU:0, one launch (start us, length us, event | category | flops | bytes accessed | tf_op | source)
XLA Modules:
  0.0 188.4 jit_solution(7670630454433331770)
XLA Ops:
  0.6 0.5 multiply_power_fusion.freq_ref
  1.2 182.9 %layer.1 = (bf16[128,1024]{1,0:T(8,128)(2,1)}, bf16[128,1024]{1,0:T(8,128)(2,1)}, f32[64,4096]{1,0:T(8,128)}, f32[64,6144]{1,0:T(8,128)}, f32[128,1024]{1,0:T(8,...) custom-call(s32[1,128]{1,0:T(1,128)} %pos_ref.1, f32[1,64]{1,0:T(1,128)} %multiply_power_fusion.freq_ref, ...), custom_call_target="tpu_custom_call" | custom-call | tf_op jit(solution)/shard_map/layer/pallas_call | solution.py:718
  184.0 4.4 %deliver.1 = (bf16[128,1024]{1,0:T(8,128)(2,1)}, bf16[128,1024]{1,0:T(8,128)(2,1)}, f32[64,2048]{1,0:T(8,128)}, f32[64,1024]{1,0:T(8,128)}, f32[64,1024]{1,0:T(8...) custom-call(bf16[128,1024]{1,0:T(8,128)(2,1)} %get-tuple-element.33., ...), custom_call_target="tpu_custom_call" | custom-call | tf_op jit(solution)/shard_map/deliver/pallas_call | solution.py:778

commit v7 on v6

--- a/solution.py
+++ b/solution.py
@@ -223,7 +223,8 @@
 
 def layer_kernel(
     pos_ref, freq_ref, n1_ref, n2_ref, qn_ref, kn_ref, x_ref, dy_ref, wq, wk, wv, wo, wg, wu, wd,
-    y_ref, dh_ref, oqkv, ogu, owo, owd, ogain,
+    y_out, dh_out, oqkv, ogu, wo_out, wd_out, gain_out,
+    y_ref, dh_ref, owo, owd, ogain,
     gains, gbuf, bq, bk, bv, bo, bg, bu, bd, g1, g2,
     xp, trig, n_s, q_s, k_s, v_s, qr, kr, probs, ctx, h_s, m_s, spare, act, dact, dctx, dres,
     part_a, part_y, part_m, part_n, land_a, land_y, land_m, land_n,
@@ -286,6 +287,12 @@
     gain_number, norm_number = 9, 10
     sent = []
 
+    leaving = []
+
+    def leave(buf, out):
+        leaving.append(pltpu.make_async_copy(buf, out, local_sem.at[len(parts) + 2 + len(leaving)]))
+        leaving[-1].start()
+
     def near_copy(dim, source, target):
         number = len(sent)
         sent.append(
@@ -310,7 +317,7 @@
     def _(k):
         pl.semaphore_signal(barrier, inc=1, device_id=other(k + 1), device_id_type=MESH)
 
-    gains[...] = jnp.zeros((8, 128), F32)
+    gains[...] = jnp.zeros(gains.shape, F32)
     halves = [ref[...].astype(F32).reshape(1, 64) for ref in (n1_ref, n2_ref)]
     gains[0:1, :] = jnp.concatenate(halves, axis=1)
     gains[1:2, :] = qn_ref[...].astype(F32).reshape(1, 128)
@@ -638,13 +645,14 @@
         return total + jnp.sum(grad * unit, axis=0, keepdims=True)
 
     d_g1 = loop(4, d_hidden_rows, jnp.zeros((1, D), F32))
+    leave(dh_ref, dh_out)
+    gpart[...] = jnp.zeros(gpart.shape, F32)
     for i in range(8):
         tile = slice(128 * i, 128 * i + 128)
         gpart[i : i + 1, :] = d_g1[:, tile]
         gpart[8 + i : 9 + i, :] = d_g2[:, tile]
     gpart[16:17, :] = q_total
     gpart[17:18, :] = k_total
-    gpart[18:24, :] = jnp.zeros((6, 128), F32)
 
     to_all(gpart, gainbuf, gain_number)
     received(y_copies)
@@ -654,6 +662,8 @@
         rows = cols(i, 32)
         out = (part_y[z, rows] + land_y[rows]).astype(BF16).astype(F32)
         y_ref[rows] = (h_s[rows] + out).astype(BF16)
+
+    leave(y_ref, y_out)
 
     def final(dim, number, result, target, out, chunk, base):
         group = Group(place, tuple(k for k in range(4) if k != dim))
@@ -680,8 +690,10 @@
             moves.append(final(X, 7 + chunk, rqkv, zqkv, oqkv, chunk, qkv_base))
     wd_far.wait_recv()
     owd[...] = rwd[x] + zwd[...]
+    leave(owd, wd_out)
     wo_far.wait_recv()
     owo[...] = rwo[y] + zwo[...]
+    leave(owo, wo_out)
     all_wait(gainbuf, one_recv.at[gain_number])
     gainbuf[me] = gpart[...]
     gainbuf[0] = loop(16, lambda i, total: total + gainbuf[i], jnp.zeros((24, 128), F32)) * inv_tokens
@@ -690,12 +702,15 @@
         ogain[i : i + 1, :] = jnp.where(c == 0, row, pltpu.roll(row, 64, axis=1))
     ogain[2:4, :] = gainbuf[0, 16:18, :]
     ogain[4:8, :] = jnp.zeros((4, 128), F32)
+    leave(ogain, gain_out)
     for move in moves:
         move.arrived()
     for item in moves + [e_gu, e_qkv, e_a, e_c] + parts:
         item.drain()
     for copy in sent:
         copy.wait_send()
+    for copy in leaving:
+        copy.wait()
     all_wait(gainbuf, one_send.at[gain_number])
     all_wait(gbuf, one_send.at[norm_number])
 
@@ -723,8 +738,9 @@
             shape(128, D, F32), shape(192, D, F32), shape(8, 128, F32),
         ),
         in_specs=[vmem] * 6 + [hbm] * 9,
-        out_specs=(vmem, vmem, hbm, hbm, vmem, vmem, vmem),
+        out_specs=(hbm,) * 7,
         scratch_shapes=[
+            *many(2, (T, D), BF16), VM((T, D), F32), VM((192, D), F32), VM((8, 128), F32),
             VM((8, 128), F32), VM((16, 8, 128), F32), VM(cube + (64, D), BF16), *many(2, cube + (64, kvh), BF16),
             VM(square + (128, D), BF16), *many(2, cube + (64, fh), BF16), VM(square + (192, D), BF16),
             *many(2, (1, D), F32),
@@ -738,7 +754,7 @@
             VM((3,) + cube + (64, 256), F32), VM((2,) + cube + (64, 256), F32), VM((2, 192, D), F32),
             VM((2, 128, D), F32), VM((3,) + square + (64, 256), F32), VM((2,) + square + (64, 256), F32),
             VM((192, D), F32), VM((128, D), F32), VM((16, 24, 128), F32),
-            *[dma((spreads, 3))] * 2, *[dma((spreads, 4))] * 2, dma((spreads + 2,)), *[dma((11,))] * 3, *[dma((20,))] * 2,
+            *[dma((spreads, 3))] * 2, *[dma((spreads, 4))] * 2, dma((spreads + 7,)), *[dma((11,))] * 3, *[dma((20,))] * 2,
         ],
         compiler_params=pltpu.CompilerParams(collective_id=0, has_side_effects=True, vmem_limit_bytes=HIGH_VMEM),
     )(*operands)

time: 189 us -> 187 us (0.989)
  no operation moved by 1% of the time
where the time goes in v7:
time: 187 us
  Pallas kernels  186 us (99%)
    pallas_call x1, Pallas kernels, layer_call(): pl.pallas_call(layer_kernel, name='layer', out_shape=(shape(T, D, BF16),...  182 us
    pallas_call x1, Pallas kernels, deliver(): pl.pallas_call(deliver_kernel, name='deliver', out_shape=tuple([shape(*si...  4.37 us

profile of v7, /device:TPU:0, one launch (start us, length us, event | category | flops | bytes accessed | tf_op | source)
XLA Modules:
  0.0 187.3 jit_solution(16717918234958488108)
XLA Ops:
  0.6 0.5 multiply_power_fusion.freq_ref
  1.2 181.7 %layer.1 = (bf16[128,1024]{1,0:T(8,128)(2,1)}, bf16[128,1024]{1,0:T(8,128)(2,1)}, f32[64,4096]{1,0:T(8,128)}, f32[64,6144]{1,0:T(8,128)}, f32[128,1024]{1,0:T(8,...) custom-call(s32[1,128]{1,0:T(1,128)} %pos_ref.1, f32[1,64]{1,0:T(1,128)} %multiply_power_fusion.freq_ref, ...), custom_call_target="tpu_custom_call" | custom-call | tf_op jit(solution)/shard_map/layer/pallas_call | solution.py:733
  182.9 4.4 %deliver.1 = (bf16[128,1024]{1,0:T(8,128)(2,1)}, bf16[128,1024]{1,0:T(8,128)(2,1)}, f32[64,2048]{1,0:T(8,128)}, f32[64,1024]{1,0:T(8,128)}, f32[64,1024]{1,0:T(8...) custom-call(bf16[128,1024]{1,0:T(8,128)(2,1)} %get-tuple-element.33., ...), custom_call_target="tpu_custom_call" | custom-call | tf_op jit(solution)/shard_map/deliver/pallas_call | solution.py:794

commit v8 on v7

--- a/solution.py
+++ b/solution.py
@@ -618,6 +618,12 @@
         column_chunk(mbuf, gubuf, rgu, chunk)
         gu_far.append(near_copy(Y, half_of(Y, rgu, chunk), zgu.at[chunk]))
         gu_far[-1].start()
+    p_dr.advance(0)
+    p_dr.arrived()
+    e_c.arrived()
+    row_tiles(cbuf, drbuf, rwo)
+    wo_far = near_copy(Y, rwo.at[1 - y], zwo)
+    wo_far.start()
     p_n.advance(0)
     p_n.arrived()
     e_qkv.arrived()
@@ -626,13 +632,6 @@
         column_chunk(nbuf, qkvbuf, rqkv, chunk)
         qkv_far.append(near_copy(X, half_of(X, rqkv, chunk), zqkv.at[chunk]))
         qkv_far[-1].start()
-    p_dr.advance(0)
-    p_dr.arrived()
-    e_c.arrived()
-    row_tiles(cbuf, drbuf, rwo)
-    wo_far = near_copy(Y, rwo.at[1 - y], zwo)
-    wo_far.start()
-
     received(n_copies)
 
     def d_hidden_rows(i, total):

time: 187 us -> 187 us (level)
  no operation moved by 1% of the time
where the time goes in v8:
time: 187 us
  Pallas kernels  186 us (99%)
    pallas_call x1, Pallas kernels, layer_call(): pl.pallas_call(layer_kernel, name='layer', out_shape=(shape(T, D, BF16),...  182 us
    pallas_call x1, Pallas kernels, deliver(): pl.pallas_call(deliver_kernel, name='deliver', out_shape=tuple([shape(*si...  4.37 us

profile of v8, /device:TPU:0, one launch (start us, length us, event | category | flops | bytes accessed | tf_op | source)
XLA Modules:
  0.0 187.3 jit_solution(3603622182478253746)
XLA Ops:
  0.6 0.5 multiply_power_fusion.freq_ref
  1.2 181.7 %layer.1 = (bf16[128,1024]{1,0:T(8,128)(2,1)}, bf16[128,1024]{1,0:T(8,128)(2,1)}, f32[64,4096]{1,0:T(8,128)}, f32[64,6144]{1,0:T(8,128)}, f32[128,1024]{1,0:T(8,...) custom-call(s32[1,128]{1,0:T(1,128)} %pos_ref.1, f32[1,64]{1,0:T(1,128)} %multiply_power_fusion.freq_ref, ...), custom_call_target="tpu_custom_call" | custom-call | tf_op jit(solution)/shard_map/layer/pallas_call | solution.py:732
  182.9 4.4 %deliver.1 = (bf16[128,1024]{1,0:T(8,128)(2,1)}, bf16[128,1024]{1,0:T(8,128)(2,1)}, f32[64,2048]{1,0:T(8,128)}, f32[64,1024]{1,0:T(8,128)}, f32[64,1024]{1,0:T(8...) custom-call(bf16[128,1024]{1,0:T(8,128)(2,1)} %get-tuple-element.33., ...), custom_call_target="tpu_custom_call" | custom-call | tf_op jit(solution)/shard_map/deliver/pallas_call | solution.py:793
